TPU v7x, 32 devices: a whole 2x2x4 slice. The times are simulated.
32 devices in a mesh: dp: 8 (over z, x), fsdp: 4 (over y, core).
Axes of the slice: x: 2, y: 2, z: 4, core: 2. Of those that a mesh axis runs over, the one named last changes fastest.
Arguments:
- tokens: int32 [32768], P(('dp', 'fsdp')), may hold values from 0 to 50687
- lengths: int32 [32], P(('dp', 'fsdp')), may hold values from 256 to 1024, as said below
- loss_picks: int32 [32, 64], P(('dp', 'fsdp')), may hold values from 0 to 1048575
- embedding: bfloat16 [50688, 1024], P('fsdp'), may hold values from -0.359375 to 0.359375
- in_weight: bfloat16 [1024, 4384], P('fsdp'), may hold values from -0.1875 to 0.1875
- out_weight: bfloat16 [2048, 1024], P('fsdp'), may hold values from -0.125 to 0.125
- ahead_weight: bfloat16 [1024, 1024], P('fsdp'), may hold values from -0.1875 to 0.1875
- conv_weight: bfloat16 [5, 2304], P(None, 'fsdp'), may hold values from -3 to 3
- head_params: bfloat16 [3, 32], P(None, 'fsdp'), may hold values from -6 to 1.5, as said below
- norm_gains: bfloat16 [4096], P('fsdp'), may hold values from 0.5 to 1.5
- table_rows: float32 [50688], P('fsdp'), may hold values from 1e-16 to 5e-09
- table_columns: float32 [1024], P('dp'), may hold values from 3e-10 to 5e-09
- in_rows: float32 [1024], P('fsdp'), may hold values from 3e-10 to 5e-09
- in_columns: float32 [4384], replicated, may hold values from 3e-10 to 5e-09
- out_rows: float32 [2048], P('fsdp'), may hold values from 3e-10 to 5e-09
- out_columns: float32 [1024], replicated, may hold values from 3e-10 to 5e-09
- ahead_rows: float32 [1024], P('fsdp'), may hold values from 3e-10 to 5e-09
- ahead_columns: float32 [1024], replicated, may hold values from 3e-10 to 5e-09
- conv_moment: float32 [5, 2304], P(None, 'fsdp'), may hold values from 3e-10 to 5e-09
- head_moment: float32 [3, 32], P(None, 'fsdp'), may hold values from 3e-10 to 5e-09
- gain_moment: float32 [4096], P('fsdp'), may hold values from 3e-10 to 5e-09
Outputs:
- new_table: float32 [50688, 1024], P('fsdp', 'dp')
- new_in_weight: float32 [1024, 4384], P('fsdp')
- new_out_weight: float32 [2048, 1024], P('fsdp')
- new_ahead_weight: float32 [1024, 1024], P('fsdp')
- new_conv_weight: float32 [5, 2304], P(None, 'fsdp')
- new_head_params: float32 [3, 32], P(None, 'fsdp')
- new_norm_gains: float32 [4096], P('fsdp')
- new_table_rows: float32 [50688], P('fsdp')
- new_table_columns: float32 [1024], P('dp')
- new_in_rows: float32 [1024], P('fsdp')
- new_in_columns: float32 [4384], replicated
- new_out_rows: float32 [2048], P('fsdp')
- new_out_columns: float32 [1024], replicated
- new_ahead_rows: float32 [1024], P('fsdp')
- new_ahead_columns: float32 [1024], replicated
- new_conv_moment: float32 [5, 2304], P(None, 'fsdp')
- new_head_moment: float32 [3, 32], P(None, 'fsdp')
- new_gain_moment: float32 [4096], P('fsdp')
- loss: float32 [], replicated
- grad_norm: float32 [], replicated
Inputs may be any that keep to these rules, and one draw needn't show every extreme that they name: `lengths`: some sequence has all 1024 slots valid. `head_params`: row 0 lies in -6 to -3, row 1 in -2.31 to 1.39, row 2 in 0.5 to 1.5.
All inputs are finite; a program needn't handle non-finite values.
Results may differ from a plain program's by a relative error of at most 0.0045.
Values may be sent and summed in bfloat16 or wider, within the bound.
A program may use at most 384 MiB of HBM per device.

v0:
```python
import jax
import jax.numpy as jnp
from jax import lax
from jax.sharding import PartitionSpec as P

D = 1024
HEADS = 32
HEAD_DIM = 64
STATE = 128
VOCAB = 50688
KERNEL = 4
SPAN = 256
INNER = 2048
CONV_WIDTH = 2304
IN_WIDTH = 4384
GAINS = 4096


PRECISE = lax.Precision.HIGHEST
EPSILON = 1e-05
DECAY_RATE = 0.5
STEP_RATE = 0.2
CLIP_NORM = 0.2
AFTER_SHARE = 0.3
FLOOR_RMS = 0.001
MASK_FILL = -10000.0


def merged_2(value, axis, join):
    pieces = jax.tree.map(lambda part: lax.all_gather(part, axis), value)
    head = jax.tree.map(lambda part: part[0], pieces)
    tail = jax.tree.map(lambda part: part[1:], pieces)
    running, _ = lax.scan(lambda running, piece: (join(running, piece), None), head, tail)
    return running


def rms_norm(values_in, gain_in):
    return (
        values_in
        * lax.rsqrt(jnp.mean(values_in * values_in, axis=-1, keepdims=True) + EPSILON)
        * gain_in
    )


def block_step(carried, pieces):
    block_x, block_steps, block_rates, block_keys, block_queries = pieces
    log_decay = jnp.cumsum(block_rates, axis=0)
    row_index = jnp.arange(block_rates.shape[0])
    causal = row_index[:, None] >= row_index[None, :]
    decay_grid = jnp.exp(
        jnp.where(causal[:, :, None], log_decay[:, None, :] - log_decay[None, :, :], MASK_FILL)
    )
    scores = jnp.dot(block_queries, block_keys.T, precision=PRECISE)
    mix_weights = scores[:, :, None] * decay_grid * block_steps[None, :, :]
    within = jnp.einsum("tsh,shp->thp", mix_weights, block_x, precision=PRECISE)
    from_state = jnp.exp(log_decay)[:, :, None] * jnp.einsum(
        "tn,hpn->thp", block_queries, carried, precision=PRECISE
    )
    tail_decay = jnp.exp(log_decay[-1][None, :] - log_decay) * block_steps
    carried = jnp.exp(log_decay[-1])[:, None, None] * carried + jnp.einsum(
        "sh,shp,sn->hpn", tail_decay, block_x, block_keys, precision=PRECISE
    )
    return (carried, within + from_state)


def state_mixer(projected, conv_table, head_table, gain_in):
    length = projected.shape[0]
    gate_part = projected[:, :INNER]
    conv_input = projected[:, INNER : INNER + CONV_WIDTH]
    step_raw = projected[:, INNER + CONV_WIDTH :]
    padded = jnp.concatenate([jnp.zeros((KERNEL - 1, CONV_WIDTH), jnp.float32), conv_input], axis=0)
    conv_sum = conv_table[KERNEL]
    for offset in range(KERNEL):
        conv_sum = conv_sum + conv_table[offset] * padded[offset : offset + length]
    activated = jax.nn.silu(conv_sum)
    x_heads = activated[:, :INNER].reshape(length, HEADS, HEAD_DIM)
    key_part = activated[:, INNER : INNER + STATE]
    query_part = activated[:, INNER + STATE :]
    step_size = jax.nn.softplus(step_raw + head_table[0])
    rates = -step_size * jnp.exp(head_table[1])
    blocks = length // SPAN
    initial = jnp.zeros((HEADS, HEAD_DIM, STATE), jnp.float32)
    _, head_out = lax.scan(
        jax.checkpoint(block_step),
        initial,
        (
            x_heads.reshape(blocks, SPAN, HEADS, HEAD_DIM),
            step_size.reshape(blocks, SPAN, HEADS),
            rates.reshape(blocks, SPAN, HEADS),
            key_part.reshape(blocks, SPAN, STATE),
            query_part.reshape(blocks, SPAN, STATE),
        ),
    )
    head_out = head_out.reshape(length, HEADS, HEAD_DIM) + head_table[2][None, :, None] * x_heads
    gated = head_out.reshape(length, INNER) * jax.nn.silu(gate_part)
    return rms_norm(gated, gain_in)


def contract(one_side, other_side, one_dim, other_dim):
    return lax.dot_general(
        one_side,
        other_side,
        (((one_dim,), (other_dim,)), ((), ())),
        preferred_element_type=jnp.float32,
    )


def run_layer(embedded, gathered):
    in_matrix, out_matrix, ahead_matrix, conv_table, head_table, gain_table = gathered
    gain_values = gain_table.astype(jnp.float32)
    normed, pull_pre = jax.vjp(rms_norm, embedded, gain_values[:D])
    normed_low = normed.astype(jnp.bfloat16)
    projected = jnp.dot(normed_low, in_matrix, preferred_element_type=jnp.float32)
    mixed, pull_mix = jax.vjp(
        state_mixer,
        projected,
        conv_table.astype(jnp.float32),
        head_table.astype(jnp.float32),
        gain_values[D + D :],
    )
    mixed_low = mixed.astype(jnp.bfloat16)
    residual = embedded + jnp.dot(mixed_low, out_matrix, preferred_element_type=jnp.float32)
    final_norm, pull_final = jax.vjp(rms_norm, residual, gain_values[D : D + D])
    return (normed_low, mixed_low, final_norm, pull_pre, pull_mix, pull_final)


def shard_terms(logits, local_target):
    row_max = jnp.max(logits, axis=1)
    exp_total = jnp.sum(jnp.exp(logits - row_max[:, None]), axis=1)
    onehot = (jnp.arange(logits.shape[1])[None, :] == local_target[:, None]).astype(jnp.float32)
    picked = jnp.sum(onehot * logits, axis=1)
    return (row_max, exp_total, picked, onehot)


def combine_totals(one_side, other_side):
    combined = []
    for base in (0, 3):
        row_max = jnp.maximum(one_side[base], other_side[base])
        exp_total = one_side[base + 1] * jnp.exp(one_side[base] - row_max) + other_side[
            base + 1
        ] * jnp.exp(other_side[base] - row_max)
        combined = combined + [row_max, exp_total, one_side[base + 2] + other_side[base + 2]]
    return tuple(combined)


def shards(
    tokens,
    lengths,
    loss_picks,
    embedding,
    in_weight,
    out_weight,
    ahead_weight,
    conv_weight,
    head_params,
    norm_gains,
    table_rows,
    table_columns,
    in_rows,
    in_columns,
    out_rows,
    out_columns,
    ahead_rows,
    ahead_columns,
    conv_moment,
    head_moment,
    gain_moment,
):
    group_size = lax.axis_size("fsdp")
    my_rank = lax.axis_index("fsdp")
    replica_count = lax.axis_size("dp")
    replica_rank = lax.axis_index("dp")
    seq_len = tokens.shape[0]
    places = loss_picks[0] % (lengths[0] - 2)
    loss_rows = places.shape[0]
    packed = jnp.concatenate([tokens, tokens[places + 1], tokens[places + 2]])
    group_ids = lax.all_gather(packed, "fsdp", axis=0, tiled=True).reshape(
        group_size, seq_len + 2 * loss_rows
    )
    all_tokens = group_ids[:, :seq_len].reshape(-1)
    next_ids = group_ids[:, seq_len : seq_len + loss_rows].reshape(-1)
    after_ids = group_ids[:, seq_len + loss_rows :].reshape(-1)
    vocab_part = embedding.shape[0]
    width_total = embedding.shape[1]
    column_part = width_total // replica_count
    first_id = my_rank * vocab_part
    local_ids = all_tokens - first_id
    inside = (local_ids >= 0) & (local_ids < vocab_part)
    safe_ids = jnp.clip(local_ids, 0, vocab_part - 1)
    looked = jnp.where(inside[:, None], embedding[safe_ids], jnp.zeros((), jnp.bfloat16)).astype(
        jnp.float32
    )
    embedded = lax.psum_scatter(
        looked.astype(jnp.bfloat16), "fsdp", scatter_dimension=0, tiled=True
    ).astype(jnp.float32)
    gathered = (
        lax.all_gather(in_weight, "fsdp", axis=0, tiled=True),
        lax.all_gather(out_weight, "fsdp", axis=0, tiled=True),
        lax.all_gather(ahead_weight, "fsdp", axis=0, tiled=True),
        lax.all_gather(conv_weight, "fsdp", axis=1, tiled=True),
        lax.all_gather(head_params, "fsdp", axis=1, tiled=True),
        lax.all_gather(norm_gains, "fsdp", axis=0, tiled=True),
    )
    normed_low, mixed_low, final_norm, pull_pre, pull_mix, pull_final = run_layer(
        embedded, gathered
    )
    first_low = final_norm[places].astype(jnp.bfloat16)
    second_low = jnp.dot(first_low, gathered[2], preferred_element_type=jnp.float32).astype(
        jnp.bfloat16
    )
    group_first, group_second = (
        lax.all_gather(first_low, "fsdp", axis=0, tiled=True),
        lax.all_gather(second_low, "fsdp", axis=0, tiled=True),
    )
    logits_next = contract(group_first, embedding, 1, 1)
    logits_after = contract(group_second, embedding, 1, 1)
    max_next, sum_next, pick_next, hot_next = shard_terms(logits_next, next_ids - first_id)
    max_after, sum_after, pick_after, hot_after = shard_terms(logits_after, after_ids - first_id)
    merged = merged_2(
        (max_next, sum_next, pick_next, max_after, sum_after, pick_after), "fsdp", combine_totals
    )
    lse_next = merged[0] + jnp.log(merged[1])
    lse_after = merged[3] + jnp.log(merged[4])
    count_all = loss_rows * group_size * replica_count
    group_loss = (
        jnp.sum(lse_next - merged[2]) + AFTER_SHARE * jnp.sum(lse_after - merged[5])
    ) / count_all
    grad_next = ((jnp.exp(logits_next - lse_next[:, None]) - hot_next) / count_all).astype(
        jnp.bfloat16
    )
    grad_after = (
        (jnp.exp(logits_after - lse_after[:, None]) - hot_after) * (AFTER_SHARE / count_all)
    ).astype(jnp.bfloat16)
    gathered = (
        lax.all_gather(in_weight, "fsdp", axis=0, tiled=True),
        lax.all_gather(out_weight, "fsdp", axis=0, tiled=True),
        lax.all_gather(ahead_weight, "fsdp", axis=0, tiled=True),
        lax.all_gather(conv_weight, "fsdp", axis=1, tiled=True),
        lax.all_gather(head_params, "fsdp", axis=1, tiled=True),
        lax.all_gather(norm_gains, "fsdp", axis=0, tiled=True),
    )
    normed_low, mixed_low, final_norm, pull_pre, pull_mix, pull_final = run_layer(
        embedded, gathered
    )
    in_matrix, out_matrix, ahead_matrix = (gathered[0], gathered[1], gathered[2])
    rows_next_grad = contract(grad_next, embedding, 1, 0)
    rows_after_grad = contract(grad_after, embedding, 1, 0)
    d_first_own, d_second_own = (
        lax.psum_scatter(rows_next_grad, "fsdp", scatter_dimension=0, tiled=True),
        lax.psum_scatter(rows_after_grad, "fsdp", scatter_dimension=0, tiled=True),
    )
    d_second = d_second_own.astype(jnp.bfloat16)
    d_ahead = contract(first_low, d_second, 0, 0)
    d_first = d_first_own + contract(d_second, ahead_matrix, 1, 1)
    d_final = jnp.zeros_like(final_norm).at[places].add(d_first)
    d_residual, d_gain_final = pull_final(d_final)
    d_out = d_residual.astype(jnp.bfloat16)
    d_out_weight = contract(mixed_low, d_out, 0, 0)
    d_mixed = contract(d_out, out_matrix, 1, 1)
    d_projected, d_conv, d_heads, d_gain_mix = pull_mix(d_mixed)
    d_projected_low = d_projected.astype(jnp.bfloat16)
    d_in_weight = contract(normed_low, d_projected_low, 0, 0)
    d_normed = contract(d_projected_low, in_matrix, 1, 1)
    d_pre, d_gain_first = pull_pre(d_normed)
    d_embedded = d_residual + d_pre
    group_grads = lax.all_gather(
        d_embedded.astype(jnp.bfloat16), "fsdp", axis=0, tiled=True
    ).astype(d_embedded.dtype)
    masked_grads = jnp.where(inside[:, None], group_grads, 0.0)
    d_gains = jnp.concatenate([d_gain_first, d_gain_final, d_gain_mix])
    shares = (
        lax.psum_scatter(d_in_weight, "fsdp", scatter_dimension=0, tiled=True),
        lax.psum_scatter(d_out_weight, "fsdp", scatter_dimension=0, tiled=True),
        lax.psum_scatter(d_ahead, "fsdp", scatter_dimension=0, tiled=True),
        lax.psum_scatter(d_conv, "fsdp", scatter_dimension=1, tiled=True),
        lax.psum_scatter(d_heads, "fsdp", scatter_dimension=1, tiled=True),
        lax.psum_scatter(d_gains, "fsdp", scatter_dimension=0, tiled=True),
    )
    d_table = contract(grad_next, group_first, 0, 0) + contract(grad_after, group_second, 0, 0)
    d_table = d_table.at[safe_ids].add(masked_grads)
    table_own = lax.psum_scatter(
        d_table.astype(jnp.bfloat16), "dp", scatter_dimension=1, tiled=True
    ).astype(jnp.float32)
    summed = lax.psum(
        (shares[0], shares[1], shares[2], shares[3], shares[4], shares[5], group_loss), "dp"
    )
    gradients = [table_own] + list(summed[:6])
    loss = summed[6]
    column_start = replica_rank * column_part
    row_start = my_rank * vocab_part
    table_old = lax.dynamic_slice_in_dim(embedding, column_start, column_part, 1).astype(
        jnp.float32
    )
    olds = [table_old] + [
        weight.astype(jnp.float32)
        for weight in (in_weight, out_weight, ahead_weight, conv_weight, head_params, norm_gains)
    ]
    replicated = 1.0 / replica_count
    weight_shares = (1.0,) + (replicated,) * 6
    element_counts = (
        VOCAB * D,
        D * IN_WIDTH,
        INNER * D,
        D * D,
        (KERNEL + 1) * CONV_WIDTH,
        3 * HEADS,
        GAINS,
    )
    row_counts = (VOCAB, D, INNER, D)
    row_olds = (table_rows, in_rows, out_rows, ahead_rows)
    column_olds = (table_columns, in_columns, out_columns, ahead_columns)
    norm_part = sum(
        (share * jnp.sum(gradient * gradient) for share, gradient in zip(weight_shares, gradients))
    )
    weight_squares = jnp.stack(
        [share * jnp.sum(weight * weight) for share, weight in zip(weight_shares, olds)]
    )
    norm_total, weight_total = lax.psum((norm_part, weight_squares), ("dp", "fsdp"))
    grad_norm = jnp.sqrt(norm_total)
    factor = jnp.minimum(1.0, CLIP_NORM / grad_norm)
    clipped = [gradient * factor for gradient in gradients]
    table_squared = clipped[0] * clipped[0]
    other_rows = [
        DECAY_RATE * row_olds[position]
        + (1.0 - DECAY_RATE) * jnp.mean(clipped[position] * clipped[position], axis=1)
        for position in range(1, 4)
    ]
    row_sums = jnp.stack(
        [
            DECAY_RATE * replicated * jnp.sum(table_rows)
            + (1.0 - DECAY_RATE) * jnp.sum(table_squared) / D
        ]
        + [replicated * jnp.sum(row_state) for row_state in other_rows]
    )
    column_totals = lax.psum(
        (
            lax.dynamic_update_slice(
                jnp.zeros((width_total,), jnp.float32),
                jnp.sum(table_squared, axis=0),
                (column_start,),
            ),
            replicated * jnp.sum(clipped[1] * clipped[1], axis=0),
            replicated * jnp.sum(clipped[2] * clipped[2], axis=0),
            replicated * jnp.sum(clipped[3] * clipped[3], axis=0),
            lax.dynamic_update_slice(
                jnp.zeros((vocab_part * group_size,), jnp.float32),
                jnp.sum(table_squared, axis=1),
                (row_start,),
            ),
            row_sums,
        ),
        ("dp", "fsdp"),
    )
    rows_new = [
        DECAY_RATE * table_rows
        + (1.0 - DECAY_RATE)
        * lax.dynamic_slice_in_dim(column_totals[4], row_start, vocab_part, 0)
        / D
    ] + other_rows
    columns_new = [
        DECAY_RATE * table_columns
        + (1.0 - DECAY_RATE)
        * lax.dynamic_slice_in_dim(column_totals[0], column_start, column_part, 0)
        / VOCAB
    ] + [
        DECAY_RATE * column_olds[position]
        + (1.0 - DECAY_RATE) * column_totals[position] / row_counts[position]
        for position in range(1, 4)
    ]
    row_means = [column_totals[5][position] / row_counts[position] for position in range(4)]
    step_sizes = [
        STEP_RATE
        * jnp.maximum(FLOOR_RMS, jnp.sqrt(weight_total[position] / element_counts[position]))
        for position in range(7)
    ]
    new_weights = []
    for position in range(4):
        estimate = (
            rows_new[position][:, None] * columns_new[position][None, :] / row_means[position]
        )
        new_weights.append(
            olds[position] - step_sizes[position] * clipped[position] * lax.rsqrt(estimate)
        )
    new_moments = []
    for position, old_moment in zip(range(4, 7), (conv_moment, head_moment, gain_moment)):
        moment_new = (
            DECAY_RATE * old_moment + (1.0 - DECAY_RATE) * clipped[position] * clipped[position]
        )
        new_moments.append(moment_new)
        new_weights.append(
            olds[position] - step_sizes[position] * clipped[position] * lax.rsqrt(moment_new)
        )
    return (
        new_weights[0],
        new_weights[1],
        new_weights[2],
        new_weights[3],
        new_weights[4],
        new_weights[5],
        new_weights[6],
        rows_new[0],
        columns_new[0],
        rows_new[1],
        columns_new[1],
        rows_new[2],
        columns_new[2],
        rows_new[3],
        columns_new[3],
        new_moments[0],
        new_moments[1],
        new_moments[2],
        loss,
        grad_norm,
    )


def solution(mesh):
    in_specs = (
        P(("dp", "fsdp")),
        P(("dp", "fsdp")),
        P(("dp", "fsdp"), None),
        P("fsdp", None),
        P("fsdp", None),
        P("fsdp", None),
        P("fsdp", None),
        P(None, "fsdp"),
        P(None, "fsdp"),
        P("fsdp"),
        P("fsdp"),
        P("dp"),
        P("fsdp"),
        P(),
        P("fsdp"),
        P(),
        P("fsdp"),
        P(),
        P(None, "fsdp"),
        P(None, "fsdp"),
        P("fsdp"),
    )
    out_specs = (
        P("fsdp", "dp"),
        P("fsdp", None),
        P("fsdp", None),
        P("fsdp", None),
        P(None, "fsdp"),
        P(None, "fsdp"),
        P("fsdp"),
        P("fsdp"),
        P("dp"),
        P("fsdp"),
        P(),
        P("fsdp"),
        P(),
        P("fsdp"),
        P(),
        P(None, "fsdp"),
        P(None, "fsdp"),
        P("fsdp"),
        P(),
        P(),
    )
    return jax.shard_map(shards, mesh=mesh, in_specs=in_specs, out_specs=out_specs, check_vma=False)
```

profile of v0, /device:TPU:0, one launch (start us, length us, event | category | flops | bytes accessed | tf_op | source)
XLA Modules:
  0.0 2985.4 jit_solution(16358210636527006372)
XLA Ops:
  19.4 32.6 %gather_fusion.2 = bf16[4096,1024]{1,0:T(8,128)(2,1)} fusion(bf16[12672,1024]{1,0:T(8,128)(2,1)} %param.32, s32[4096]{0:T(1024)S(1)} %broadcast_clamp_fusion), kind=kCustom, calls=%fused_computation.2 | custom fusion | bytes 16793600 | tf_op jit(solution)/shard_map/gather | solution.py:190
  52.0 11.3 copy.332
  93.8 50.3 %reduce-scatter.14.cloned.1.call-done = bf16[1024,1024]{0,1:T(8,128)(2,1)} async-done(((bf16[4096,1024]{0,1:T(8,128)(2,1)}), bf16[1024,1024]{0,1:T(8,128)(2,1)}) %reduce-scatter.14.cloned.1.call-update) | async-done | bytes 2097168 | tf_op jit(solution)/shard_map/reduce_scatter | solution.py:193
  146.2 62.3 %all-gather.20.cloned.1.call-done = bf16[1024,4384]{0,1:T(8,128)(2,1)} async-done(((bf16[256,4384]{0,1:T(8,128)(2,1)}), bf16[1024,4384]{0,1:T(8,128)(2,1)}) %all-gather.20.cloned.1.call-update) | async-done | bytes 8978448 | tf_op jit(solution)/shard_map/all_gather | solution.py:197
  208.5 16.8 fusion.168
  230.1 12.3 fusion.132
  277.0 279.5 %while.76 = (s32[]{:T(128)}, f32[32,64,128]{2,1,0:T(8,128)}, f32[4,256,32,64]{1,0,3,2:T(4,128)}, f32[4,256,32]{1,2,0:T(8,128)}, f32[4,256,32]{1,2,0:T(8,128)S(1)...) while((s32[]{:T(128)}, f32[32,64,128]{2,1,0:T(8,128)}, ...), condition=%wide.region_13.14_spmd.clone, body=%wide.region_10.13_spmd.clone.sunk | while | flops 3333971968 | bytes 23665168 | solution.py:83
  280.4 11.1 fusion.301
  296.4 45.7 %dynamic_update_slice.92 = f32[4,256,32,64]{1,0,3,2:T(4,128)} dynamic-update-slice(f32[4,256,32,64]{1,0,3,2:T(4,128)} %get-tuple-element.1574, f32[1,256,32,64]{1,0,3,2:T(1,128)S(1)} %copy.554, s32[]{:T(128)} %get-tuple-element.1572, s32[]{:T(128)} %constant.296.clone.1..sunk, s32[]{:T(128)} %constant.296.clone.1..sunk, s32[]{:T(128)} %constant.296.clone.1..sunk) | dynamic-update-slice | bytes 4194308 | tf_op jit(solution)/shard_map/jvp()/while/body/jit(dynamic_update_index_in_dim)/dynamic_update_slice | solution.py:83
  349.7 11.1 fusion.301
  366.1 45.7 %dynamic_update_slice.92 = f32[4,256,32,64]{1,0,3,2:T(4,128)} dynamic-update-slice(f32[4,256,32,64]{1,0,3,2:T(4,128)} %get-tuple-element.1574, f32[1,256,32,64]{1,0,3,2:T(1,128)S(1)} %copy.554, s32[]{:T(128)} %get-tuple-element.1572, s32[]{:T(128)} %constant.296.clone.1..sunk, s32[]{:T(128)} %constant.296.clone.1..sunk, s32[]{:T(128)} %constant.296.clone.1..sunk) | dynamic-update-slice | bytes 4194308 | tf_op jit(solution)/shard_map/jvp()/while/body/jit(dynamic_update_index_in_dim)/dynamic_update_slice | solution.py:83
  419.7 11.1 fusion.301
  436.1 45.7 %dynamic_update_slice.92 = f32[4,256,32,64]{1,0,3,2:T(4,128)} dynamic-update-slice(f32[4,256,32,64]{1,0,3,2:T(4,128)} %get-tuple-element.1574, f32[1,256,32,64]{1,0,3,2:T(1,128)S(1)} %copy.554, s32[]{:T(128)} %get-tuple-element.1572, s32[]{:T(128)} %constant.296.clone.1..sunk, s32[]{:T(128)} %constant.296.clone.1..sunk, s32[]{:T(128)} %constant.296.clone.1..sunk) | dynamic-update-slice | bytes 4194308 | tf_op jit(solution)/shard_map/jvp()/while/body/jit(dynamic_update_index_in_dim)/dynamic_update_slice | solution.py:83
  489.7 11.1 fusion.301
  506.1 45.7 %dynamic_update_slice.92 = f32[4,256,32,64]{1,0,3,2:T(4,128)} dynamic-update-slice(f32[4,256,32,64]{1,0,3,2:T(4,128)} %get-tuple-element.1574, f32[1,256,32,64]{1,0,3,2:T(1,128)S(1)} %copy.554, s32[]{:T(128)} %get-tuple-element.1572, s32[]{:T(128)} %constant.296.clone.1..sunk, s32[]{:T(128)} %constant.296.clone.1..sunk, s32[]{:T(128)} %constant.296.clone.1..sunk) | dynamic-update-slice | bytes 4194308 | tf_op jit(solution)/shard_map/jvp()/while/body/jit(dynamic_update_index_in_dim)/dynamic_update_slice | solution.py:83
  570.5 279.3 %while.77 = (s32[]{:T(128)}, f32[32,64,128]{2,1,0:T(8,128)S(1)}, f32[4,256,32,64]{1,0,3,2:T(4,128)}, f32[4,32,64,128]{3,2,1,0:T(8,128)}, f32[4,256,32]{1,2,0:T(8...) while((s32[]{:T(128)}, f32[32,64,128]{2,1,0:T(8,128)S(1)}, ...), condition=%wide.region_30.31_spmd.clone, body=%wide.region_27.30_spmd.clone.sunk | while | flops 3334234112 | bytes 25762840 | solution.py:83
  574.0 11.1 fusion.312
  590.0 45.7 %dynamic_update_slice.94 = f32[4,256,32,64]{1,0,3,2:T(4,128)} dynamic-update-slice(f32[4,256,32,64]{1,0,3,2:T(4,128)} %get-tuple-element.1536, f32[1,256,32,64]{1,0,3,2:T(1,128)S(1)} %copy.558, s32[]{:T(128)} %get-tuple-element.1534, s32[]{:T(128)} %constant.296.clone.1..sunk.1, s32[]{:T(128)} %constant.296.clone.1..sunk.1, s32[]{:T(128)} %constant.296.clone.1..sunk.1) | dynamic-update-slice | bytes 4194308 | tf_op jit(solution)/shard_map/jvp()/while/body/jit(dynamic_update_index_in_dim)/dynamic_update_slice | solution.py:83
  643.7 11.1 fusion.312
  659.7 45.7 %dynamic_update_slice.94 = f32[4,256,32,64]{1,0,3,2:T(4,128)} dynamic-update-slice(f32[4,256,32,64]{1,0,3,2:T(4,128)} %get-tuple-element.1536, f32[1,256,32,64]{1,0,3,2:T(1,128)S(1)} %copy.558, s32[]{:T(128)} %get-tuple-element.1534, s32[]{:T(128)} %constant.296.clone.1..sunk.1, s32[]{:T(128)} %constant.296.clone.1..sunk.1, s32[]{:T(128)} %constant.296.clone.1..sunk.1) | dynamic-update-slice | bytes 4194308 | tf_op jit(solution)/shard_map/jvp()/while/body/jit(dynamic_update_index_in_dim)/dynamic_update_slice | solution.py:83
  713.5 11.1 fusion.312
  729.5 45.7 %dynamic_update_slice.94 = f32[4,256,32,64]{1,0,3,2:T(4,128)} dynamic-update-slice(f32[4,256,32,64]{1,0,3,2:T(4,128)} %get-tuple-element.1536, f32[1,256,32,64]{1,0,3,2:T(1,128)S(1)} %copy.558, s32[]{:T(128)} %get-tuple-element.1534, s32[]{:T(128)} %constant.296.clone.1..sunk.1, s32[]{:T(128)} %constant.296.clone.1..sunk.1, s32[]{:T(128)} %constant.296.clone.1..sunk.1) | dynamic-update-slice | bytes 4194308 | tf_op jit(solution)/shard_map/jvp()/while/body/jit(dynamic_update_index_in_dim)/dynamic_update_slice | solution.py:83
  783.3 11.1 fusion.312
  799.3 45.7 %dynamic_update_slice.94 = f32[4,256,32,64]{1,0,3,2:T(4,128)} dynamic-update-slice(f32[4,256,32,64]{1,0,3,2:T(4,128)} %get-tuple-element.1536, f32[1,256,32,64]{1,0,3,2:T(1,128)S(1)} %copy.558, s32[]{:T(128)} %get-tuple-element.1534, s32[]{:T(128)} %constant.296.clone.1..sunk.1, s32[]{:T(128)} %constant.296.clone.1..sunk.1, s32[]{:T(128)} %constant.296.clone.1..sunk.1) | dynamic-update-slice | bytes 4194308 | tf_op jit(solution)/shard_map/jvp()/while/body/jit(dynamic_update_index_in_dim)/dynamic_update_slice | solution.py:83
  855.6 19.7 multiply_reduce_fusion.11
  899.6 12.2 fusion.210
  938.8 12.3 fusion.209
  976.2 19.7 fusion.192
  996.6 20.3 fusion.190
  1025.0 11.6 multiply_reduce_fusion.18
  1036.6 12.4 reduce-scatter.16.cloned.1.call-done
  1067.8 14.3 multiply_reduce_fusion.8
  1082.2 16.6 multiply_reduce_fusion.9
  1098.7 10.5 reshape.618
  1109.3 12.5 fusion.162
  1130.2 596.5 %while.78 = (s32[]{:T(128)}, f32[32,64,128]{2,1,0:T(8,128)}, f32[4,256,32,64]{1,0,3,2:T(4,128)}, f32[4,256,32]{2,1,0:T(8,128)}, f32[4,256,32]{1,0,2:T(4,128)}, /...) while((s32[]{:T(128)}, f32[32,64,128]{2,1,0:T(8,128)}, ...), condition=%wide.region_47.48_spmd.clone, body=%wide.region_35.47_spmd.clone.sunk | while | flops 7593680896 | bytes 63674056 | solution.py:83
  1183.4 15.4 fusion.334
  1235.2 45.8 %dynamic_update_slice.98 = f32[4,256,32,64]{1,0,3,2:T(4,128)} dynamic-update-slice(f32[4,256,32,64]{1,0,3,2:T(4,128)} %get-tuple-element.1658, f32[1,256,32,64]{1,0,3,2:T(1,128)} %copy.572, s32[]{:T(128)S(6)} %sub.496, s32[]{:T(128)} %constant.296.clone.1..sunk.2, s32[]{:T(128)} %constant.296.clone.1..sunk.2, s32[]{:T(128)} %constant.296.clone.1..sunk.2) | dynamic-update-slice | bytes 4194308 | tf_op jit(solution)/shard_map/transpose(jvp())/while/body/jit(dynamic_update_index_in_dim)/dynamic_update_slice | solution.py:83
  1326.2 15.4 fusion.334
  1377.9 45.8 %dynamic_update_slice.98 = f32[4,256,32,64]{1,0,3,2:T(4,128)} dynamic-update-slice(f32[4,256,32,64]{1,0,3,2:T(4,128)} %get-tuple-element.1658, f32[1,256,32,64]{1,0,3,2:T(1,128)} %copy.572, s32[]{:T(128)S(6)} %sub.496, s32[]{:T(128)} %constant.296.clone.1..sunk.2, s32[]{:T(128)} %constant.296.clone.1..sunk.2, s32[]{:T(128)} %constant.296.clone.1..sunk.2) | dynamic-update-slice | bytes 4194308 | tf_op jit(solution)/shard_map/transpose(jvp())/while/body/jit(dynamic_update_index_in_dim)/dynamic_update_slice | solution.py:83
  1468.9 15.4 fusion.334
  1520.7 45.8 %dynamic_update_slice.98 = f32[4,256,32,64]{1,0,3,2:T(4,128)} dynamic-update-slice(f32[4,256,32,64]{1,0,3,2:T(4,128)} %get-tuple-element.1658, f32[1,256,32,64]{1,0,3,2:T(1,128)} %copy.572, s32[]{:T(128)S(6)} %sub.496, s32[]{:T(128)} %constant.296.clone.1..sunk.2, s32[]{:T(128)} %constant.296.clone.1..sunk.2, s32[]{:T(128)} %constant.296.clone.1..sunk.2) | dynamic-update-slice | bytes 4194308 | tf_op jit(solution)/shard_map/transpose(jvp())/while/body/jit(dynamic_update_index_in_dim)/dynamic_update_slice | solution.py:83
  1611.7 15.4 fusion.334
  1663.4 45.8 %dynamic_update_slice.98 = f32[4,256,32,64]{1,0,3,2:T(4,128)} dynamic-update-slice(f32[4,256,32,64]{1,0,3,2:T(4,128)} %get-tuple-element.1658, f32[1,256,32,64]{1,0,3,2:T(1,128)} %copy.572, s32[]{:T(128)S(6)} %sub.496, s32[]{:T(128)} %constant.296.clone.1..sunk.2, s32[]{:T(128)} %constant.296.clone.1..sunk.2, s32[]{:T(128)} %constant.296.clone.1..sunk.2) | dynamic-update-slice | bytes 4194308 | tf_op jit(solution)/shard_map/transpose(jvp())/while/body/jit(dynamic_update_index_in_dim)/dynamic_update_slice | solution.py:83
  1749.7 26.7 multiply_reduce_fusion.7
  1776.5 10.5 broadcast_multiply_fusion
  1787.0 14.6 pad_add_fusion
  1801.6 19.3 fusion.166
  1821.0 18.8 fusion.148
  1849.8 104.3 %reduce-scatter.20.cloned.1.call-done = f32[256,4384]{0,1:T(8,128)} async-done(((f32[1024,4384]{0,1:T(8,128)}), f32[256,4384]{0,1:T(8,128)}) %reduce-scatter.20.cloned.1.call-update) | async-done | bytes 4489232 | tf_op jit(solution)/shard_map/reduce_scatter | solution.py:272
  1954.3 27.9 fusion.191
  1982.2 39.0 %convolution_add_fusion.2 = f32[12672,1024]{1,0:T(8,128)} fusion(f32[12672,1024]{1,0:T(8,128)} %fusion.191, bf16[256,1024]{1,0:T(8,128)(2,1)S(1)} %copy-done.19, f32[256,12672]{1,0:T(8,128)} %copy-done.4, f32[256]{0:T(256)S(1)} %copy-done.67, s32[256]{0:T(256)S(1)} %copy-done.61), kind=kOutput, calls=%fused_computation.186 | convolution fusion | flops 6676217856 | bytes 117311488 | tf_op jit(solution)/shard_map/dot_general | solution.py:100
  2021.2 11.9 convert_select_fusion
  2033.1 17.6 copy.363
  2050.7 70.6 %scatter_fusion = f32[12672,1024]{1,0:T(8,128)} fusion(f32[12672,1024]{1,0:T(8,128)} %convolution_add_fusion.2, s32[4096]{0:T(1024)S(1)} %bitcast.575, f32[4096,1024]{1,0:T(8,128)} %copy.363), kind=kCustom, calls=%fused_computation.5 | custom fusion | flops 4194304 | bytes 50348032 | tf_op jit(solution)/shard_map/scatter-add | solution.py:280
  2121.3 26.7 convert_element_type.112
  2148.0 31.1 %copy.379 = bf16[12672,1024]{0,1:T(8,128)(2,1)} copy(bf16[12672,1024]{1,0:T(8,128)(2,1)} %convert_element_type.112) | data formatting | bytes 51904512
  2198.4 10.8 all-reduce.26
  2210.4 39.4 %all-reduce.24 = (f32[5,576]{1,0:T(8,128)S(1)}, f32[3,8]{1,0:T(4,128)S(1)}, f32[1024]{0:T(1024)S(1)}, f32[]{:T(128)}) all-reduce(f32[5,576]{1,0:T(8,128)S(1)} %copy.382, f32[3,8]{1,0:T(4,128)S(1)} %constant_dynamic-slice_fusion.8, f32[1024]{0:T(1024)S(1)} %dynamic-slice.3, f32[]{:T(128)S(6)} %div.218), channel_id=1, replica_groups=mesh['dp'=8,'fsdp'=4] {'dp'}, use_global_device_ids=true, to_apply=%region_67.68 | all-reduce | flops 3929 | bytes 31432 | tf_op jit(solution)/shard_map/psum | solution.py:284
  2253.5 43.5 %all-reduce.32.cloned.1.call-done = (f32[256,1024]{1,0:T(8,128)}, f32[256,4384]{0,1:T(8,128)}, f32[512,1024]{1,0:T(8,128)}) async-done(((f32[256,1024]{1,0:T(8,128)}, f32[256,4384]{0,1:T(8,128)}, f32[512,1024]{1,0:T(8,128)}), (f32[256,1024]{1,0:T(8,128)}, f32[256,4384]{0,1:T(8,128)}, f32[512,1024]{1,0:T(8,128)})) %all-reduce.32.cloned.1.call-update) | async-done | bytes 7634960 | tf_op jit(solution)/shard_map/psum | solution.py:284
  2307.9 406.9 %reduce-scatter.26.cloned.1.call-done = bf16[128,12672]{1,0:T(8,128)(2,1)} async-done(((bf16[1024,12672]{1,0:T(8,128)(2,1)}), bf16[128,12672]{1,0:T(8,128)(2,1)}) %reduce-scatter.26.cloned.1.call-update) | async-done | bytes 3244048
  2723.6 39.2 %psum.112 = f32[]{:T(128)} all-reduce(f32[]{:T(128)S(6)} %add.499), channel_id=1, replica_groups=mesh['dp'=8,'fsdp'=4] {'dp','fsdp'}, use_global_device_ids=true, to_apply=%region_82.83 | all-reduce | flops 1 | bytes 8 | tf_op jit(solution)/shard_map/psum | solution.py:318
  2781.7 116.1 %all-reduce.30.cloned.1.call-done = f32[50688]{0:T(1024)} async-done(((f32[50688]{0:T(1024)}), f32[50688]{0:T(1024)}) %all-reduce.30.cloned.1.call-update) | async-done | bytes 202768 | tf_op jit(solution)/shard_map/psum | solution.py:335
  2900.0 41.9 %all-reduce.23 = (f32[4]{0:T(128)S(1)}, f32[1024]{0:T(1024)S(1)}, f32[7]{0:T(128)S(1)}, f32[4384]{0:T(1024)S(1)}, f32[1024]{0:T(1024)S(1)}, /*index=5*/f32[1024]{0:T(1024)S(1)}) all-reduce(f32[4]{0:T(128)S(1)} %pad_maximum_fusion.1, f32[1024]{0:T(1024)S(1)} %dynamic_update_slice.71, ...), channel_id=1, replica_groups=mesh['dp'=8,'fsdp'=4] {'dp','fsdp'}, use_global_device_ids=true, to_apply=%region_95.96 | all-reduce | flops 7467 | bytes 59736 | tf_op jit(solution)/shard_map/psum | solution.py:335
  (762 shorter events, 754.3 us)
Async XLA Ops:
  7.2 136.9 %reduce-scatter.14.cloned.1.call-start = ((), (), s32[]{:S(2)}) async-start(), calls=%async_computation.8 | async-start | bytes 10485760 | tf_op jit(solution)/shard_map/reduce_scatter | solution.py:193
  8.7 83.2 %copy-start.90 = (s32[64]{0:T(128)}, s32[64]{0:T(128)S(1)}, u32[]{:S(2)}) copy-start(s32[64]{0:T(128)S(1)} %get-tuple-element.1088) | copy-start | bytes 772
  71.0 137.5 %all-gather.20.cloned.1.call-start = ((), (), s32[]{:S(2)}) async-start(), calls=%async_computation.9 | async-start | bytes 11223040 | tf_op jit(solution)/shard_map/all_gather | solution.py:197
  71.8 803.6 %all-gather.22.cloned.1.call-start = ((), (), s32[]{:S(2)}) async-start(), calls=%async_computation.10 | async-start | bytes 5242880 | tf_op jit(solution)/shard_map/all_gather | solution.py:198
  72.5 817.5 %all-gather.24.cloned.1.call-start = ((), (), s32[]{:S(2)}) async-start(), calls=%async_computation.11 | async-start | bytes 2621440 | tf_op jit(solution)/shard_map/all_gather | solution.py:199
  73.1 948.1 %reduce-scatter.18.cloned.1.call-start = ((), (), s32[]{:S(2)}) async-start(), calls=%async_computation.13 | async-start | bytes 1310720 | tf_op jit(solution)/shard_map/reduce_scatter | solution.py:250
  79.2 146.1 %copy-start.70 = (f32[1024]{0:T(1024)}, f32[1024]{0:T(1024)S(1)}, u32[]{:S(2)}) copy-start(f32[1024]{0:T(1024)S(1)} %get-tuple-element.1130) | copy-start | bytes 12292
  85.3 144.7 %copy-start.37 = (f32[2304]{0:T(1024)}, f32[2304]{0:T(1024)S(1)}, u32[]{:S(2)}) copy-start(f32[2304]{0:T(1024)S(1)} %get-tuple-element.944) | copy-start | bytes 27652
  85.3 144.7 %copy-start.39 = (f32[2304]{0:T(1024)}, f32[2304]{0:T(1024)S(1)}, u32[]{:S(2)}) copy-start(f32[2304]{0:T(1024)S(1)} %get-tuple-element.945) | copy-start | bytes 27652
  85.4 144.7 %copy-start.41 = (f32[2304]{0:T(1024)}, f32[2304]{0:T(1024)S(1)}, u32[]{:S(2)}) copy-start(f32[2304]{0:T(1024)S(1)} %get-tuple-element.946) | copy-start | bytes 27652
  85.4 144.7 %copy-start.43 = (f32[2304]{0:T(1024)}, f32[2304]{0:T(1024)S(1)}, u32[]{:S(2)}) copy-start(f32[2304]{0:T(1024)S(1)} %get-tuple-element.947) | copy-start | bytes 27652
  91.1 178.1 %copy-start.80 = (f32[32]{0:T(128)}, f32[32]{0:T(128)S(1)}, u32[]{:S(2)}) copy-start(f32[32]{0:T(128)S(1)} %get-tuple-element.1132) | copy-start | bytes 388
  91.1 178.1 %copy-start.82 = (f32[32]{0:T(128)}, f32[32]{0:T(128)S(1)}, u32[]{:S(2)}) copy-start(f32[32]{0:T(128)S(1)} %get-tuple-element.1133) | copy-start | bytes 388
  146.1 79.2 %copy-start.54 = (f32[1024]{0:T(1024)}, f32[1024]{0:T(1024)S(1)}, u32[]{:S(2)}) copy-start(f32[1024]{0:T(1024)S(1)} %fusion.152) | copy-start | bytes 12292
  146.2 79.2 %copy-start.68 = (f32[1024]{0:T(1024)}, f32[1024]{0:T(1024)S(1)}, u32[]{:S(2)}) copy-start(f32[1024]{0:T(1024)S(1)} %fusion.180) | copy-start | bytes 12292
  855.5 19.8 copy-start.2
  855.6 19.8 copy-start.9
  855.6 19.8 copy-start.59
  911.8 19.3 copy-start.4
  921.0 30.2 %copy-start.50 = (f32[4,1,256]{2,1,0:T(1,128)}, f32[4,1,256]{2,1,0:T(1,128)S(1)}, u32[]{:S(2)}) copy-start(f32[4,1,256]{2,1,0:T(1,128)S(1)} %all-gather.13) | copy-start | bytes 12292
  926.0 25.2 copy-start.49
  931.1 20.1 copy-start.51
  951.2 23.9 slice-start.5
  951.2 23.9 slice-start.7
  951.2 23.9 slice-start.9
  951.2 24.0 slice-start.6
  951.2 24.0 slice-start.8
  951.2 24.0 slice-start.10
  976.2 19.7 copy-start.66
  996.0 53.0 %reduce-scatter.16.cloned.1.call-start = ((), (), s32[]{:S(2)}) async-start(), calls=%async_computation.12 | async-start | bytes 1310720 | tf_op jit(solution)/shard_map/reduce_scatter | solution.py:249
  996.6 20.3 copy-start.62
  996.6 20.4 copy-start.25
  996.6 24.6 copy-start.23
  1017.0 832.8 %reduce-scatter.24.cloned.1.call-start = ((), (), s32[]{:S(2)}) async-start(), calls=%async_computation.17 | async-start | bytes 5242880 | tf_op jit(solution)/shard_map/reduce_scatter | solution.py:274
  1024.9 824.9 %reduce-scatter.22.cloned.1.call-start = ((), (), s32[]{:S(2)}) async-start(), calls=%async_computation.16 | async-start | bytes 10485760 | tf_op jit(solution)/shard_map/reduce_scatter | solution.py:273
  1024.9 24.1 copy-start.30
  1121.8 832.3 %reduce-scatter.20.cloned.1.call-start = ((), (), s32[]{:S(2)}) async-start(), calls=%async_computation.15 | async-start | bytes 22446080 | tf_op jit(solution)/shard_map/reduce_scatter | solution.py:272
  1222.6 58.5 %copy-start.15 = (f32[256,32]{1,0:T(8,128)S(1)}, f32[256,32]{1,0:T(8,128)}, u32[]{:S(2)}) copy-start(f32[256,32]{1,0:T(8,128)} %get-tuple-element.1519) | copy-start | bytes 98308 | tf_op jit(solution)/shard_map/transpose(jvp())/while
  1365.3 58.5 %copy-start.15 = (f32[256,32]{1,0:T(8,128)S(1)}, f32[256,32]{1,0:T(8,128)}, u32[]{:S(2)}) copy-start(f32[256,32]{1,0:T(8,128)} %get-tuple-element.1519) | copy-start | bytes 98308 | tf_op jit(solution)/shard_map/transpose(jvp())/while
  1508.1 58.5 %copy-start.15 = (f32[256,32]{1,0:T(8,128)S(1)}, f32[256,32]{1,0:T(8,128)}, u32[]{:S(2)}) copy-start(f32[256,32]{1,0:T(8,128)} %get-tuple-element.1519) | copy-start | bytes 98308 | tf_op jit(solution)/shard_map/transpose(jvp())/while
  1650.8 58.5 %copy-start.15 = (f32[256,32]{1,0:T(8,128)S(1)}, f32[256,32]{1,0:T(8,128)}, u32[]{:S(2)}) copy-start(f32[256,32]{1,0:T(8,128)} %get-tuple-element.1519) | copy-start | bytes 98308 | tf_op jit(solution)/shard_map/transpose(jvp())/while
  1749.7 26.7 copy-start.38
  1749.7 26.7 copy-start.40
  1749.7 26.8 copy-start.42
  1749.7 26.8 copy-start.44
  1821.0 200.2 %all-gather.26.cloned.1.call-start = ((), (), s32[]{:S(2)}) async-start(), calls=%async_computation.14 | async-start | bytes 10485760 | tf_op jit(solution)/shard_map/all_gather | solution.py:266
  1848.0 106.2 %copy-start.20 = (bf16[256,1024]{1,0:T(8,128)(2,1)S(1)}, bf16[256,1024]{1,0:T(8,128)(2,1)}, u32[]{:S(2)}) copy-start(bf16[256,1024]{1,0:T(8,128)(2,1)} %all_gather.78) | copy-start | bytes 1572868
  1848.0 106.2 %copy-start.53 = (s32[256]{0:T(256)S(1)}, s32[256]{0:T(256)}, u32[]{:S(2)}) copy-start(s32[256]{0:T(256)} %sub.271) | copy-start | bytes 3076
  1848.0 106.2 %copy-start.63 = (f32[256]{0:T(256)S(1)}, f32[256]{0:T(256)}, u32[]{:S(2)}) copy-start(f32[256]{0:T(256)} %copy-done.62) | copy-start | bytes 3076
  1848.1 361.2 %reduce-scatter.28.cloned.1.call-start = ((), (), s32[]{:S(2)}) async-start(), calls=%async_computation.20 | async-start | bytes 1474560
  1849.7 447.3 %all-reduce.32.cloned.1.call-start = ((), (), s32[]{:S(2)}) async-start(), calls=%async_computation.21 | async-start | bytes 15269888 | tf_op jit(solution)/shard_map/psum | solution.py:284
  1954.2 28.0 copy-start.19
  1954.2 28.0 copy-start.61
  1954.2 28.0 copy-start.67
  1954.2 760.5 %reduce-scatter.26.cloned.1.call-start = ((), (), s32[]{:S(2)}) async-start(), calls=%async_computation.19 | async-start | bytes 29196288
  1982.2 39.0 %copy-start.57 = (pred[1,8,4,128]{3,1,2,0:T(8,128)(4,1)S(1)}, pred[1,8,4,128]{3,1,2,0:T(8,128)(4,1)}, u32[]{:S(2)}) copy-start(pred[1,8,4,128]{3,1,2,0:T(8,128)(4,1)} %copy-done.56) | copy-start | bytes 12292
  2179.2 718.6 %all-reduce.30.cloned.1.call-start = ((), (), s32[]{:S(2)}) async-start(), calls=%async_computation.18 | async-start | bytes 409600 | tf_op jit(solution)/shard_map/psum | solution.py:335
  2249.7 472.0 %copy-start.75 = (f32[1024]{0:T(1024)}, f32[1024]{0:T(1024)S(1)}, u32[]{:S(2)}) copy-start(f32[1024]{0:T(1024)S(1)} %get-tuple-element.1048) | copy-start | bytes 12292
  2249.7 472.0 %copy-start.77 = (f32[3,8]{1,0:T(4,128)}, f32[3,8]{1,0:T(4,128)S(1)}, u32[]{:S(2)}) copy-start(f32[3,8]{1,0:T(4,128)S(1)} %get-tuple-element.1047) | copy-start | bytes 292
  2775.6 193.4 %copy-start.85 = (f32[256]{0:T(256)}, f32[256]{0:T(256)S(1)}, u32[]{:S(2)}) copy-start(f32[256]{0:T(256)S(1)} %get-tuple-element.1072) | copy-start | bytes 3076
  2776.9 192.1 %copy-start.76 = (f32[512]{0:T(512)}, f32[512]{0:T(512)S(1)}, u32[]{:S(2)}) copy-start(f32[512]{0:T(512)S(1)} %get-tuple-element.1074) | copy-start | bytes 6148
  2778.2 190.8 %copy-start.84 = (f32[256]{0:T(256)}, f32[256]{0:T(256)S(1)}, u32[]{:S(2)}) copy-start(f32[256]{0:T(256)S(1)} %get-tuple-element.1076) | copy-start | bytes 3076
  2899.3 69.7 %copy-start.32 = (f32[12672]{0:T(1024)}, f32[12672]{0:T(1024)S(1)}, u32[]{:S(2)}) copy-start(f32[12672]{0:T(1024)S(1)} %get-tuple-element.1125) | copy-start | bytes 152068
  2942.0 22.1 copy-start.8
  (64 other events, 667.8 us)
Sparse Core Ops, SparseCore 0:
  71.1 72.8 reduce-scatter.13
  145.6 62.8 all-gather.19
  210.0 34.4 all-gather.21
  245.9 22.5 all-gather.23
  996.1 25.0 reduce-scatter.17
  1024.2 24.7 reduce-scatter.15
  1051.5 44.5 reduce-scatter.23
  1121.9 72.3 reduce-scatter.21
  1821.1 133.0 reduce-scatter.19
  1956.1 58.2 all-gather.25
  2017.6 25.5 reduce-scatter.27
  2047.5 249.4 all-reduce.31
  2300.9 413.7 reduce-scatter.25
  2773.0 124.6 all-reduce.29
where the time goes:
time: 3010 us; the launch traced here: 2990 us
  local copies, waits for them, and re-layouts  925 us (31%)
  waiting for transfers between devices  801 us (27%)
  matrix products  603 us (20%)
  other arithmetic  388 us (13%)
  blocking collectives  199 us (7%)
  between operations  40.2 us (1%)
    dynamic_update_slice x32, local copies, waits for them, and re-layouts, state_mixer(): lax.scan(jax.checkpoint(block_step), initial, (x_heads.reshape(blocks, SP...  587 us
    unnamed x16, waiting for transfers between devices  409 us
    dot_general x12, matrix products, contract(): lax.dot_general(one_side, other_side, (((one_dim,), (other_dim,)), ((), (...  202 us
    dot_general x16, matrix products, block_step(): within = jnp.einsum('tsh,shp->thp', mix_weights, block_x, precision=PRECISE)  187 us
    psum x1, waiting for transfers between devices, shards(): lax.psum((lax.dynamic_update_slice(jnp.zeros((width_total,), jnp.float32)...  116 us
    reduce_scatter x1, waiting for transfers between devices, shards(): lax.psum_scatter(d_in_weight, 'fsdp', scatter_dimension=0, tiled=True)  104 us
    unnamed x216, local copies, waits for them, and re-layouts  84.1 us
    dot_general x16, matrix products, block_step(): jnp.einsum('sh,shp,sn->hpn', tail_decay, block_x, block_keys, precision=P...  72.5 us
  transfers between devices with their start and end apart: 14, of which 8 were waited for; matrix products, arithmetic and copies ran while one was open for 59% of the time, Pallas kernels for 0%

commit v1 on v0

v1 whole, which is shorter than its diff:
```python
import jax
import jax.numpy as jnp
from jax import lax
from jax.experimental import pallas as pl
from jax.experimental.pallas import tpu as pltpu
from jax.sharding import PartitionSpec as P

D = 1024
HEADS = 32
HEAD_DIM = 64
STATE = 128
VOCAB = 50688
KERNEL = 4
SPAN = 256
INNER = 2048
CONV_WIDTH = 2304
IN_WIDTH = 4384
GAINS = 4096
GROUP = 4
PAD = 8
CHUNK = 128


PRECISE = lax.Precision.HIGHEST
EPSILON = 1e-05
DECAY_RATE = 0.5
STEP_RATE = 0.2
CLIP_NORM = 0.2
AFTER_SHARE = 0.3
FLOOR_RMS = 0.001
MASK_FILL = -10000.0


def merged_2(value, axis, join):
    pieces = jax.tree.map(lambda part: lax.all_gather(part, axis), value)
    head = jax.tree.map(lambda part: part[0], pieces)
    tail = jax.tree.map(lambda part: part[1:], pieces)
    running, _ = lax.scan(lambda running, piece: (join(running, piece), None), head, tail)
    return running


def rms_norm(values_in, gain_in):
    return (
        values_in
        * lax.rsqrt(jnp.mean(values_in * values_in, axis=-1, keepdims=True) + EPSILON)
        * gain_in
    )


def gated_norm(head_rows, gate_rows, gain_in):
    return rms_norm(head_rows * jax.nn.silu(gate_rows), gain_in)


def contract(one_side, other_side, one_dim, other_dim):
    return lax.dot_general(
        one_side,
        other_side,
        (((one_dim,), (other_dim,)), ((), ())),
        preferred_element_type=jnp.float32,
    )


def split(value):
    high = value.astype(jnp.bfloat16)
    return high, (value - high.astype(jnp.float32)).astype(jnp.bfloat16)


def product(one_side, other_side, one_dim, other_dim):
    return lax.dot_general(
        one_side,
        other_side,
        (((one_dim,), (other_dim,)), ((), ())),
        preferred_element_type=jnp.float32,
    )


def product_3(one_side, other_side, one_dim, other_dim):
    one_high, one_low = one_side
    other_high, other_low = other_side
    return (
        product(one_high, other_high, one_dim, other_dim)
        + product(one_low, other_high, one_dim, other_dim)
        + product(one_high, other_low, one_dim, other_dim)
    )


def exact(one_side, other_side, one_dim, other_dim):
    return lax.dot_general(
        one_side,
        other_side,
        (((one_dim,), (other_dim,)), ((), ())),
        precision=PRECISE,
        preferred_element_type=jnp.float32,
    )


def running_sum(values, backward):
    length = values.shape[1]
    lane = lax.broadcasted_iota(jnp.int32, values.shape, 1)
    shift = 1
    while shift < length:
        if backward:
            moved = pltpu.roll(values, length - shift, 1)
            values = values + jnp.where(lane < length - shift, moved, 0.0)
        else:
            moved = pltpu.roll(values, shift, 1)
            values = values + jnp.where(lane >= shift, moved, 0.0)
        shift *= 2
    return values


def taps_sum(window, taps_ref, rows):
    total = taps_ref[KERNEL : KERNEL + 1, :]
    for offset in range(KERNEL):
        start = PAD - KERNEL + 1 + offset
        total = total + taps_ref[offset : offset + 1, :] * window[start : start + rows]
    return total


def sigmoid(value):
    return 1.0 / (1.0 + jnp.exp(-value))


def decay_spread(row_decay, places, lane):
    here = lane == places
    at_place = jnp.sum(jnp.where(here, row_decay, 0.0), axis=1, keepdims=True)
    return jnp.exp(jnp.where(lane <= places, at_place - row_decay, MASK_FILL)), here


def mix_forward_kernel(
    normed_ref,
    weight_ref,
    taps_ref,
    raw_ref,
    columns_ref,
    places_ref,
    skip_ref,
    input_ref,
    out_ref,
    scores_ref,
    keys_ref,
    queries_ref,
    steps_ref,
    decay_ref,
    padded,
    active,
    mix_high,
    mix_low,
):
    step = pl.program_id(0)
    length = normed_ref.shape[0]
    rows = places_ref.shape[0]
    width = weight_ref.shape[1]
    chunk = CHUNK
    places = places_ref[...]
    lane = lax.broadcasted_iota(jnp.int32, (rows, length), 1)
    value = product(normed_ref[...], weight_ref[...], 1, 0)
    input_ref[...] = value
    padded[0:PAD, :] = jnp.zeros((PAD, width), jnp.float32)
    padded[PAD:, :] = value

    def activate(index, carry):
        start = pl.multiple_of(index * chunk, chunk)
        window = padded[pl.ds(start, chunk + PAD), :]
        total = taps_sum(window, taps_ref, chunk)
        active[pl.ds(start, chunk), :] = total * sigmoid(total)
        return carry

    lax.fori_loop(0, length // chunk, activate, 0)

    @pl.when(step == 0)
    def _():
        keys = active[:, :STATE]
        keys_ref[...] = keys
        picked = exact((lane == places).astype(jnp.float32), active[:, STATE:], 1, 0)
        queries_ref[...] = picked
        scores_ref[...] = exact(picked, keys, 1, 1)
        shifted = raw_ref[...] + columns_ref[:, 0:1]
        steps = jnp.maximum(shifted, 0.0) + jnp.log1p(jnp.exp(-jnp.abs(shifted)))
        steps_ref[...] = steps
        decay_ref[...] = running_sum(-steps * jnp.exp(columns_ref[:, 1:2]), False)

    @pl.when(step > 0)
    def _():
        scores = scores_ref[...]
        for index in range(GROUP):
            head = (step - 1) * GROUP + index
            row_steps = steps_ref[pl.ds(head, 1), :]
            spread, here = decay_spread(decay_ref[pl.ds(head, 1), :], places, lane)
            weights = scores * spread * row_steps + jnp.where(here, skip_ref[head], 0.0)
            high, low = split(weights)
            mix_high[index * rows : (index + 1) * rows, :] = high
            mix_low[index * rows : (index + 1) * rows, :] = low
        x_pair = split(active[...])
        mixed = product_3((mix_high[...], mix_low[...]), x_pair, 1, 0)
        column = lax.broadcasted_iota(jnp.int32, (rows, width), 1) // HEAD_DIM
        total = jnp.zeros((rows, width), jnp.float32)
        for index in range(GROUP):
            total = jnp.where(column == index, mixed[index * rows : (index + 1) * rows], total)
        out_ref[...] = total


def mix_forward(normed, weight, taps, raw, columns, places, skip):
    length = normed.shape[0]
    rows = places.shape[0]
    width = GROUP * HEAD_DIM
    blocks = CONV_WIDTH // width
    last = blocks - 1
    whole = lambda shape: pl.BlockSpec(shape, lambda step: (0,) * len(shape))
    turned = lambda step: (0, lax.rem(step + last, blocks))
    f32 = jnp.float32
    return pl.pallas_call(
        mix_forward_kernel,
        grid=(blocks,),
        in_specs=[
            whole((length, D)),
            pl.BlockSpec((D, width), turned),
            pl.BlockSpec((KERNEL + 1, width), turned),
            whole((HEADS, length)),
            whole((HEADS, 3)),
            whole((rows, 1)),
            pl.BlockSpec(memory_space=pltpu.SMEM),
        ],
        out_specs=[
            pl.BlockSpec((length, width), turned),
            pl.BlockSpec((rows, width), lambda step: (0, jnp.maximum(step - 1, 0))),
            whole((rows, length)),
            whole((length, STATE)),
            whole((rows, STATE)),
            whole((HEADS, length)),
            whole((HEADS, length)),
        ],
        out_shape=[
            jax.ShapeDtypeStruct((length, CONV_WIDTH), f32),
            jax.ShapeDtypeStruct((rows, INNER), f32),
            jax.ShapeDtypeStruct((rows, length), f32),
            jax.ShapeDtypeStruct((length, STATE), f32),
            jax.ShapeDtypeStruct((rows, STATE), f32),
            jax.ShapeDtypeStruct((HEADS, length), f32),
            jax.ShapeDtypeStruct((HEADS, length), f32),
        ],
        scratch_shapes=[
            pltpu.VMEM((length + PAD, width), f32),
            pltpu.VMEM((length, width), f32),
            pltpu.VMEM((GROUP * rows, length), jnp.bfloat16),
            pltpu.VMEM((GROUP * rows, length), jnp.bfloat16),
        ],
        compiler_params=pltpu.CompilerParams(vmem_limit_bytes=40 << 20),
        cost_estimate=pl.CostEstimate(
            flops=2 * length * D * CONV_WIDTH * 2,
            bytes_accessed=16 << 20,
            transcendentals=HEADS * rows * length,
        ),
        name="mix_forward",
    )(normed, weight, taps, raw, columns, places, skip)


def mix_backward_kernel(
    input_ref,
    taps_ref,
    grad_ref,
    scores_ref,
    keys_ref,
    queries_ref,
    steps_ref,
    decay_ref,
    raw_ref,
    columns_ref,
    places_ref,
    skip_ref,
    d_input_ref,
    d_taps_ref,
    d_raw_ref,
    d_columns_ref,
    padded,
    active,
    d_active,
    d_padded,
    mix_high,
    mix_low,
    d_mix,
    d_scores,
    d_steps,
    from_place,
    d_skip,
):
    step = pl.program_id(0)
    last = pl.num_programs(0) - 1
    length, width = input_ref.shape
    rows = places_ref.shape[0]
    chunk = CHUNK
    count = length // chunk
    places = places_ref[...]
    lane = lax.broadcasted_iota(jnp.int32, (rows, length), 1)
    padded[0:PAD, :] = jnp.zeros((PAD, width), jnp.float32)
    padded[PAD:, :] = input_ref[...]

    @pl.when(step == 0)
    def _():
        d_scores[...] = jnp.zeros_like(d_scores)

    @pl.when(step < last)
    def _():
        def activate(index, carry):
            start = pl.multiple_of(index * chunk, chunk)
            window = padded[pl.ds(start, chunk + PAD), :]
            total = taps_sum(window, taps_ref, chunk)
            active[pl.ds(start, chunk), :] = total * sigmoid(total)
            return carry

        lax.fori_loop(0, count, activate, 0)
        x_pair = split(active[...])
        column = lax.broadcasted_iota(jnp.int32, (rows, width), 1) // HEAD_DIM
        grad = grad_ref[...]
        stacked = split(
            jnp.concatenate(
                [jnp.where(column == index, grad, 0.0) for index in range(GROUP)], axis=0
            )
        )
        d_mix[...] = product_3(stacked, x_pair, 1, 1)
        scores = scores_ref[...]
        for index in range(GROUP):
            head = step * GROUP + index
            row_steps = steps_ref[pl.ds(head, 1), :]
            spread, here = decay_spread(decay_ref[pl.ds(head, 1), :], places, lane)
            weights = scores * spread
            part = d_mix[index * rows : (index + 1) * rows, :]
            d_scores[...] += part * spread * row_steps
            shared = part * weights
            d_steps[pl.ds(head, 1), :] = jnp.sum(shared, axis=0, keepdims=True)
            row_total = jnp.sum(shared * row_steps, axis=1, keepdims=True)
            from_place[pl.ds(head, 1), :] = jnp.sum(
                jnp.where(lane <= places, row_total, 0.0), axis=0, keepdims=True
            )
            d_skip[pl.ds(head, 1), :] = jnp.sum(
                jnp.where(here, part, 0.0), axis=0, keepdims=True
            )
            full = weights * row_steps + jnp.where(here, skip_ref[head], 0.0)
            high, low = split(full)
            mix_high[index * rows : (index + 1) * rows, :] = high
            mix_low[index * rows : (index + 1) * rows, :] = low
        d_active[...] = product_3((mix_high[...], mix_low[...]), stacked, 0, 0)

    @pl.when(step == last)
    def _():
        onehot = (lane == places).astype(jnp.float32)
        d_score = d_scores[...]
        d_queries = exact(d_score, keys_ref[...], 1, 0)
        d_active[:, :STATE] = exact(d_score, queries_ref[...], 0, 0)
        d_active[:, STATE:] = exact(onehot, d_queries, 0, 0)
        steps = steps_ref[...]
        direct = d_steps[...]
        rates_scale = -jnp.exp(columns_ref[:, 1:2])
        d_rates = from_place[...] - running_sum(direct * steps, True)
        d_step = direct + d_rates * rates_scale
        d_raw = d_step * sigmoid(raw_ref[...] + columns_ref[:, 0:1])
        d_raw_ref[...] = d_raw
        d_log = jnp.sum(d_rates * steps, axis=1, keepdims=True) * rates_scale
        slot = lax.broadcasted_iota(jnp.int32, d_columns_ref.shape, 1)
        d_columns_ref[...] = jnp.where(
            slot == 0,
            jnp.sum(d_raw, axis=1, keepdims=True),
            jnp.where(slot == 1, d_log, jnp.sum(d_skip[...], axis=1, keepdims=True)),
        )

    d_padded[length:, :] = jnp.zeros((PAD, width), jnp.float32)

    def through_silu(index, carry):
        start = pl.multiple_of(index * chunk, chunk)
        window = padded[pl.ds(start, chunk + PAD), :]
        total = taps_sum(window, taps_ref, chunk)
        gate = sigmoid(total)
        d_total = d_active[pl.ds(start, chunk), :] * (gate * (1.0 + total * (1.0 - gate)))
        d_padded[pl.ds(start, chunk), :] = d_total
        sums = []
        for offset in range(KERNEL):
            begin = PAD - KERNEL + 1 + offset
            sums.append(jnp.sum(d_total * window[begin : begin + chunk], axis=0, keepdims=True))
        sums.append(jnp.sum(d_total, axis=0, keepdims=True))
        return tuple(one + other for one, other in zip(carry, sums))

    sums = lax.fori_loop(
        0, count, through_silu, tuple(jnp.zeros((1, width), jnp.float32) for _ in range(KERNEL + 1))
    )
    for offset in range(KERNEL + 1):
        d_taps_ref[offset : offset + 1, :] = sums[offset]

    def through_taps(index, carry):
        start = pl.multiple_of(index * chunk, chunk)
        window = d_padded[pl.ds(start, chunk + PAD), :]
        total = taps_ref[KERNEL - 1 : KERNEL, :] * window[:chunk]
        for offset in range(KERNEL - 1):
            begin = KERNEL - 1 - offset
            total = total + taps_ref[offset : offset + 1, :] * window[begin : begin + chunk]
        d_input_ref[pl.ds(start, chunk), :] = total.astype(d_input_ref.dtype)
        return carry

    lax.fori_loop(0, count, through_taps, 0)


def mix_backward(inputs, taps, grad, scores, keys, queries, steps, decay, raw, columns, places, skip):
    length = inputs.shape[0]
    rows = places.shape[0]
    width = GROUP * HEAD_DIM
    blocks = CONV_WIDTH // width
    whole = lambda shape: pl.BlockSpec(shape, lambda step: (0,) * len(shape))
    along = lambda step: (0, step)
    f32 = jnp.float32
    return pl.pallas_call(
        mix_backward_kernel,
        grid=(blocks,),
        in_specs=[
            pl.BlockSpec((length, width), along),
            pl.BlockSpec((KERNEL + 1, width), along),
            pl.BlockSpec((rows, width), lambda step: (0, jnp.minimum(step, blocks - 2))),
            whole((rows, length)),
            whole((length, STATE)),
            whole((rows, STATE)),
            whole((HEADS, length)),
            whole((HEADS, length)),
            whole((HEADS, length)),
            whole((HEADS, 3)),
            whole((rows, 1)),
            pl.BlockSpec(memory_space=pltpu.SMEM),
        ],
        out_specs=[
            pl.BlockSpec((length, width), along),
            pl.BlockSpec((KERNEL + 1, width), along),
            whole((HEADS, length)),
            whole((HEADS, 128)),
        ],
        out_shape=[
            jax.ShapeDtypeStruct((length, CONV_WIDTH), jnp.bfloat16),
            jax.ShapeDtypeStruct((KERNEL + 1, CONV_WIDTH), f32),
            jax.ShapeDtypeStruct((HEADS, length), f32),
            jax.ShapeDtypeStruct((HEADS, 128), f32),
        ],
        scratch_shapes=[
            pltpu.VMEM((length + PAD, width), f32),
            pltpu.VMEM((length, width), f32),
            pltpu.VMEM((length, width), f32),
            pltpu.VMEM((length + PAD, width), f32),
            pltpu.VMEM((GROUP * rows, length), jnp.bfloat16),
            pltpu.VMEM((GROUP * rows, length), jnp.bfloat16),
            pltpu.VMEM((GROUP * rows, length), f32),
            pltpu.VMEM((rows, length), f32),
            pltpu.VMEM((HEADS, length), f32),
            pltpu.VMEM((HEADS, length), f32),
            pltpu.VMEM((HEADS, length), f32),
        ],
        compiler_params=pltpu.CompilerParams(vmem_limit_bytes=48 << 20),
        cost_estimate=pl.CostEstimate(
            flops=6 * HEADS * rows * length * HEAD_DIM * 4,
            bytes_accessed=20 << 20,
            transcendentals=HEADS * rows * length,
        ),
        name="mix_backward",
    )(inputs, taps, grad, scores, keys, queries, steps, decay, raw, columns, places, skip)


def shard_terms(logits, local_target):
    row_max = jnp.max(logits, axis=1)
    exp_total = jnp.sum(jnp.exp(logits - row_max[:, None]), axis=1)
    onehot = (jnp.arange(logits.shape[1])[None, :] == local_target[:, None]).astype(jnp.float32)
    picked = jnp.sum(onehot * logits, axis=1)
    return (row_max, exp_total, picked, onehot)


def combine_totals(one_side, other_side):
    combined = []
    for base in (0, 3):
        row_max = jnp.maximum(one_side[base], other_side[base])
        exp_total = one_side[base + 1] * jnp.exp(one_side[base] - row_max) + other_side[
            base + 1
        ] * jnp.exp(other_side[base] - row_max)
        combined = combined + [row_max, exp_total, one_side[base + 2] + other_side[base + 2]]
    return tuple(combined)


def shards(
    tokens,
    lengths,
    loss_picks,
    embedding,
    in_weight,
    out_weight,
    ahead_weight,
    conv_weight,
    head_params,
    norm_gains,
    table_rows,
    table_columns,
    in_rows,
    in_columns,
    out_rows,
    out_columns,
    ahead_rows,
    ahead_columns,
    conv_moment,
    head_moment,
    gain_moment,
):
    group_size = lax.axis_size("fsdp")
    my_rank = lax.axis_index("fsdp")
    replica_count = lax.axis_size("dp")
    replica_rank = lax.axis_index("dp")
    seq_len = tokens.shape[0]
    places = loss_picks[0] % (lengths[0] - 2)
    loss_rows = places.shape[0]
    packed = jnp.concatenate([tokens, tokens[places + 1], tokens[places + 2]])
    group_ids = lax.all_gather(packed, "fsdp", axis=0, tiled=True).reshape(
        group_size, seq_len + 2 * loss_rows
    )
    all_tokens = group_ids[:, :seq_len].reshape(-1)
    next_ids = group_ids[:, seq_len : seq_len + loss_rows].reshape(-1)
    after_ids = group_ids[:, seq_len + loss_rows :].reshape(-1)
    vocab_part = embedding.shape[0]
    width_total = embedding.shape[1]
    column_part = width_total // replica_count
    first_id = my_rank * vocab_part
    local_ids = all_tokens - first_id
    inside = (local_ids >= 0) & (local_ids < vocab_part)
    safe_ids = jnp.clip(local_ids, 0, vocab_part - 1)
    looked = jnp.where(inside[:, None], embedding[safe_ids], jnp.zeros((), jnp.bfloat16)).astype(
        jnp.float32
    )
    embedded = lax.psum_scatter(
        looked.astype(jnp.bfloat16), "fsdp", scatter_dimension=0, tiled=True
    ).astype(jnp.float32)
    in_gate, in_conv, in_step, out_matrix, ahead_matrix, conv_table, head_table, gain_table = (
        lax.all_gather(in_weight[:, :INNER], "fsdp", axis=0, tiled=True),
        lax.all_gather(in_weight[:, INNER : INNER + CONV_WIDTH], "fsdp", axis=0, tiled=True),
        lax.all_gather(in_weight[:, INNER + CONV_WIDTH :], "fsdp", axis=0, tiled=True),
        lax.all_gather(out_weight, "fsdp", axis=0, tiled=True),
        lax.all_gather(ahead_weight, "fsdp", axis=0, tiled=True),
        lax.all_gather(conv_weight, "fsdp", axis=1, tiled=True).astype(jnp.float32),
        lax.all_gather(head_params, "fsdp", axis=1, tiled=True).astype(jnp.float32),
        lax.all_gather(norm_gains, "fsdp", axis=0, tiled=True).astype(jnp.float32),
    )
    normed, pull_pre = jax.vjp(rms_norm, embedded, gain_table[:D])
    normed_low = normed.astype(jnp.bfloat16)
    raw = contract(in_step, normed_low, 0, 1)
    columns = head_table.T
    place_column = places[:, None]
    inputs, head_rows, scores, keys, queries, steps, decay = mix_forward(
        normed_low, in_conv, conv_table, raw, columns, place_column, head_table[2]
    )
    embedded_rows = embedded[places]
    normed_rows, pull_rows = jax.vjp(rms_norm, embedded_rows, gain_table[:D])
    normed_rows = normed_rows.astype(jnp.bfloat16)
    gate_rows = contract(normed_rows, in_gate, 1, 0)
    mixed, pull_mix = jax.vjp(gated_norm, head_rows, gate_rows, gain_table[D + D :])
    mixed_low = mixed.astype(jnp.bfloat16)
    residual = embedded_rows + contract(mixed_low, out_matrix, 1, 0)
    final_norm, pull_final = jax.vjp(rms_norm, residual, gain_table[D : D + D])
    first_low = final_norm.astype(jnp.bfloat16)
    second_low = jnp.dot(first_low, ahead_matrix, preferred_element_type=jnp.float32).astype(
        jnp.bfloat16
    )
    group_first, group_second = (
        lax.all_gather(first_low, "fsdp", axis=0, tiled=True),
        lax.all_gather(second_low, "fsdp", axis=0, tiled=True),
    )
    logits_next = contract(group_first, embedding, 1, 1)
    logits_after = contract(group_second, embedding, 1, 1)
    max_next, sum_next, pick_next, hot_next = shard_terms(logits_next, next_ids - first_id)
    max_after, sum_after, pick_after, hot_after = shard_terms(logits_after, after_ids - first_id)
    merged = merged_2(
        (max_next, sum_next, pick_next, max_after, sum_after, pick_after), "fsdp", combine_totals
    )
    lse_next = merged[0] + jnp.log(merged[1])
    lse_after = merged[3] + jnp.log(merged[4])
    count_all = loss_rows * group_size * replica_count
    group_loss = (
        jnp.sum(lse_next - merged[2]) + AFTER_SHARE * jnp.sum(lse_after - merged[5])
    ) / count_all
    grad_next = ((jnp.exp(logits_next - lse_next[:, None]) - hot_next) / count_all).astype(
        jnp.bfloat16
    )
    grad_after = (
        (jnp.exp(logits_after - lse_after[:, None]) - hot_after) * (AFTER_SHARE / count_all)
    ).astype(jnp.bfloat16)
    rows_next_grad = contract(grad_next, embedding, 1, 0)
    rows_after_grad = contract(grad_after, embedding, 1, 0)
    d_first_own, d_second_own = (
        lax.psum_scatter(rows_next_grad, "fsdp", scatter_dimension=0, tiled=True),
        lax.psum_scatter(rows_after_grad, "fsdp", scatter_dimension=0, tiled=True),
    )
    d_second = d_second_own.astype(jnp.bfloat16)
    d_ahead = contract(first_low, d_second, 0, 0)
    d_first = d_first_own + contract(d_second, ahead_matrix, 1, 1)
    d_residual, d_gain_final = pull_final(d_first)
    d_out = d_residual.astype(jnp.bfloat16)
    d_out_weight = contract(mixed_low, d_out, 0, 0)
    d_mixed = contract(d_out, out_matrix, 1, 1)
    d_head_rows, d_gate, d_gain_mix = pull_mix(d_mixed)
    d_gate_low = d_gate.astype(jnp.bfloat16)
    d_in_gate = contract(normed_rows, d_gate_low, 0, 0)
    d_pre_rows, d_gain_rows = pull_rows(contract(d_gate_low, in_gate, 1, 1))
    d_inputs, d_conv, d_raw, d_columns = mix_backward(
        inputs,
        conv_table,
        d_head_rows,
        scores,
        keys,
        queries,
        steps,
        decay,
        raw,
        columns,
        place_column,
        head_table[2],
    )
    d_heads = d_columns[:, :3].T
    d_raw_low = d_raw.astype(jnp.bfloat16)
    d_in_conv = contract(normed_low, d_inputs, 0, 0)
    d_in_step = contract(normed_low, d_raw_low, 0, 1)
    d_normed = contract(d_inputs, in_conv, 1, 1) + contract(d_raw_low, in_step, 0, 1)
    d_pre, d_gain_first = pull_pre(d_normed)
    d_gain_first = d_gain_first + d_gain_rows
    onehot = (lax.broadcasted_iota(jnp.int32, (seq_len, loss_rows), 0) == places[None, :]).astype(
        jnp.float32
    )
    d_embedded = d_pre + jnp.dot(onehot, d_residual + d_pre_rows, precision=PRECISE)
    d_in_weight = jnp.concatenate([d_in_gate, d_in_conv, d_in_step], axis=1)
    group_grads = lax.all_gather(
        d_embedded.astype(jnp.bfloat16), "fsdp", axis=0, tiled=True
    ).astype(d_embedded.dtype)
    masked_grads = jnp.where(inside[:, None], group_grads, 0.0)
    d_gains = jnp.concatenate([d_gain_first, d_gain_final, d_gain_mix])
    shares = (
        lax.psum_scatter(d_in_weight, "fsdp", scatter_dimension=0, tiled=True),
        lax.psum_scatter(d_out_weight, "fsdp", scatter_dimension=0, tiled=True),
        lax.psum_scatter(d_ahead, "fsdp", scatter_dimension=0, tiled=True),
        lax.psum_scatter(d_conv, "fsdp", scatter_dimension=1, tiled=True),
        lax.psum_scatter(d_heads, "fsdp", scatter_dimension=1, tiled=True),
        lax.psum_scatter(d_gains, "fsdp", scatter_dimension=0, tiled=True),
    )
    d_table = contract(grad_next, group_first, 0, 0) + contract(grad_after, group_second, 0, 0)
    d_table = d_table.at[safe_ids].add(masked_grads)
    table_own = lax.psum_scatter(
        d_table.astype(jnp.bfloat16), "dp", scatter_dimension=1, tiled=True
    ).astype(jnp.float32)
    summed = lax.psum(
        (shares[0], shares[1], shares[2], shares[3], shares[4], shares[5], group_loss), "dp"
    )
    gradients = [table_own] + list(summed[:6])
    loss = summed[6]
    column_start = replica_rank * column_part
    table_old = lax.dynamic_slice_in_dim(embedding, column_start, column_part, 1).astype(
        jnp.float32
    )
    olds = [table_old] + [
        weight.astype(jnp.float32)
        for weight in (in_weight, out_weight, ahead_weight, conv_weight, head_params, norm_gains)
    ]
    element_counts = (
        VOCAB * D,
        D * IN_WIDTH,
        INNER * D,
        D * D,
        (KERNEL + 1) * CONV_WIDTH,
        3 * HEADS,
        GAINS,
    )
    row_counts = (VOCAB, D, INNER, D)
    row_olds = (table_rows, in_rows, out_rows, ahead_rows)
    column_olds = (table_columns, in_columns, out_columns, ahead_columns)
    squares = [gradient * gradient for gradient in gradients[:4]]
    table_rows_sum, table_weight = lax.psum(
        (jnp.sum(squares[0], axis=1), jnp.sum(table_old * table_old)), "dp"
    )
    own_rows = [table_rows_sum] + [jnp.sum(squares[position], axis=1) for position in range(1, 4)]
    own_totals = jnp.stack(
        [jnp.sum(row_sum) for row_sum in own_rows]
        + [jnp.sum(gradient * gradient) for gradient in gradients[4:]]
        + [table_weight]
        + [jnp.sum(weight * weight) for weight in olds[1:]]
        + [jnp.sum(row_state) for row_state in row_olds]
    )
    column_sums, totals = lax.psum(
        (tuple(jnp.sum(square, axis=0) for square in squares), own_totals), "fsdp"
    )
    weight_total = totals[7:14]
    grad_norm = jnp.sqrt(jnp.sum(totals[:7]))
    factor = jnp.minimum(1.0, CLIP_NORM / grad_norm)
    factor_squared = factor * factor
    clipped = [gradient * factor for gradient in gradients]
    column_counts = (D, IN_WIDTH, D, D)
    rows_new = [
        DECAY_RATE * row_olds[position]
        + (1.0 - DECAY_RATE) * factor_squared * own_rows[position] / column_counts[position]
        for position in range(4)
    ]
    columns_new = [
        DECAY_RATE * column_olds[position]
        + (1.0 - DECAY_RATE) * factor_squared * column_sums[position] / row_counts[position]
        for position in range(4)
    ]
    row_means = [
        (
            DECAY_RATE * totals[14 + position]
            + (1.0 - DECAY_RATE) * factor_squared * totals[position] / column_counts[position]
        )
        / row_counts[position]
        for position in range(4)
    ]
    step_sizes = [
        STEP_RATE
        * jnp.maximum(FLOOR_RMS, jnp.sqrt(weight_total[position] / element_counts[position]))
        for position in range(7)
    ]
    new_weights = []
    for position in range(4):
        estimate = (
            rows_new[position][:, None] * columns_new[position][None, :] / row_means[position]
        )
        new_weights.append(
            olds[position] - step_sizes[position] * clipped[position] * lax.rsqrt(estimate)
        )
    new_moments = []
    for position, old_moment in zip(range(4, 7), (conv_moment, head_moment, gain_moment)):
        moment_new = (
            DECAY_RATE * old_moment + (1.0 - DECAY_RATE) * clipped[position] * clipped[position]
        )
        new_moments.append(moment_new)
        new_weights.append(
            olds[position] - step_sizes[position] * clipped[position] * lax.rsqrt(moment_new)
        )
    return (
        new_weights[0],
        new_weights[1],
        new_weights[2],
        new_weights[3],
        new_weights[4],
        new_weights[5],
        new_weights[6],
        rows_new[0],
        columns_new[0],
        rows_new[1],
        columns_new[1],
        rows_new[2],
        columns_new[2],
        rows_new[3],
        columns_new[3],
        new_moments[0],
        new_moments[1],
        new_moments[2],
        loss,
        grad_norm,
    )


def solution(mesh):
    in_specs = (
        P(("dp", "fsdp")),
        P(("dp", "fsdp")),
        P(("dp", "fsdp"), None),
        P("fsdp", None),
        P("fsdp", None),
        P("fsdp", None),
        P("fsdp", None),
        P(None, "fsdp"),
        P(None, "fsdp"),
        P("fsdp"),
        P("fsdp"),
        P("dp"),
        P("fsdp"),
        P(),
        P("fsdp"),
        P(),
        P("fsdp"),
        P(),
        P(None, "fsdp"),
        P(None, "fsdp"),
        P("fsdp"),
    )
    out_specs = (
        P("fsdp", "dp"),
        P("fsdp", None),
        P("fsdp", None),
        P("fsdp", None),
        P(None, "fsdp"),
        P(None, "fsdp"),
        P("fsdp"),
        P("fsdp"),
        P("dp"),
        P("fsdp"),
        P(),
        P("fsdp"),
        P(),
        P("fsdp"),
        P(),
        P(None, "fsdp"),
        P(None, "fsdp"),
        P("fsdp"),
        P(),
        P(),
    )
    return jax.shard_map(shards, mesh=mesh, in_specs=in_specs, out_specs=out_specs, check_vma=False)
```

time: 3010 us -> 1600 us (0.53)
  local copies, waits for them, and re-layouts: 925 us -> 130 us
  matrix products: 603 us -> 197 us
  other arithmetic: 388 us -> 216 us
  Pallas kernels: 0 us -> 71.9 us
  blocking collectives: 199 us -> 131 us
    dynamic_update_slice x34 -> x0, local copies, waits for them, and re-layouts: 588 us -> none  [the longest x32 587 us: state_mixer(): lax.scan(jax.checkpoint(block_step), initial, (x_heads.reshape(blocks, SP...]
    dot_general x76 -> x2, matrix products: 401 us -> 6.43 us  [the longest x1 4.28 us: shards(): jnp.dot(onehot, d_residual + d_pre_rows, precision=PRECISE)]
    psum x1 -> x0, waiting for transfers between devices: 116 us -> none  [shards(): lax.psum((lax.dynamic_update_slice(jnp.zeros((width_total,), jnp.float32)...]
    psum x3 -> x2, blocking collectives: 121 us -> 47.4 us  [the longest x1 36.1 us: shards(): lax.psum((jnp.sum(squares[0], axis=1), jnp.sum(table_old * table_old)), '...]
    pallas_call x0 -> x2, Pallas kernels: none -> 71.9 us  [the longest x1 45.4 us: mix_backward(): pl.pallas_call(mix_backward_kernel, grid=(blocks,), in_specs=[pl.BlockSpe...]
    psum x1, waiting for transfers between devices: 43.5 us -> 111 us  [shards(): lax.psum((shares[0], shares[1], shares[2], shares[3], shares[4], shares[5...]
    reduce_sum x17 -> x7, other arithmetic: 71.5 us -> 16.9 us  [the longest x3 9.51 us: shards(): jnp.sum(squares[position], axis=1)]
    reduce_scatter x1, waiting for transfers between devices: 104 us -> 137 us  [shards(): lax.psum_scatter(d_in_weight, 'fsdp', scatter_dimension=0, tiled=True)]
  transfers between devices with their start and end apart: 14 -> 14, of which waited for: 8 -> 10; matrix products, arithmetic and copies ran while one was open for 59% -> 23% of each run, Pallas kernels for 0% -> 5%
where the time goes in v1:
time: 1600 us; the launch traced here: 1590 us
  waiting for transfers between devices  812 us (51%)
  other arithmetic  216 us (14%)
  matrix products  197 us (12%)
  blocking collectives  131 us (8%)
  local copies, waits for them, and re-layouts  130 us (8%)
  Pallas kernels  71.9 us (4%)
  between operations  30.3 us (2%)
    unnamed x16, waiting for transfers between devices  409 us
    dot_general x19, matrix products, contract(): lax.dot_general(one_side, other_side, (((one_dim,), (other_dim,)), ((), (...  190 us
    reduce_scatter x1, waiting for transfers between devices, shards(): lax.psum_scatter(d_in_weight, 'fsdp', scatter_dimension=0, tiled=True)  137 us
    psum x1, waiting for transfers between devices, shards(): lax.psum((shares[0], shares[1], shares[2], shares[3], shares[4], shares[5...  111 us
    scatter-add x1, other arithmetic, shards(): d_table = d_table.at[safe_ids].add(masked_grads)  70.7 us
    unnamed x195, local copies, waits for them, and re-layouts  63 us
    pallas_call x1, Pallas kernels, mix_backward(): pl.pallas_call(mix_backward_kernel, grid=(blocks,), in_specs=[pl.BlockSpe...  45.4 us
    reduce_scatter x1, waiting for transfers between devices, shards(): lax.psum_scatter(looked.astype(jnp.bfloat16), 'fsdp', scatter_dimension=0...  43.1 us
  transfers between devices with their start and end apart: 14, of which 10 were waited for; matrix products, arithmetic and copies ran while one was open for 23% of the time, Pallas kernels for 5%

profile of v1, /device:TPU:0, one launch (start us, length us, event | category | flops | bytes accessed | tf_op | source)
XLA Modules:
  0.0 1588.4 jit_solution(6427976147092933923)
XLA Ops:
  13.1 6.3 all-gather.6
  19.5 32.6 %gather_fusion.2 = bf16[4096,1024]{1,0:T(8,128)(2,1)} fusion(bf16[12672,1024]{1,0:T(8,128)(2,1)} %param.26, s32[4096]{0:T(1024)S(1)} %broadcast_clamp_fusion), kind=kCustom, calls=%fused_computation.2 | custom fusion | bytes 16793600 | tf_op jit(solution)/shard_map/gather | solution.py:524
  52.2 7.2 broadcast_select_fusion
  59.5 3.0 copy.93
  67.3 5.4 all_gather.73
  72.8 5.1 all-gather.8
  78.7 5.2 all-gather.7
  84.1 5.8 all_gather.76
  89.9 43.1 %reduce-scatter.13.cloned.1.call-done = bf16[1024,1024]{1,0:T(8,128)(2,1)} async-done(((bf16[4096,1024]{1,0:T(8,128)(2,1)}), bf16[1024,1024]{1,0:T(8,128)(2,1)}) %reduce-scatter.13.cloned.1.call-update) | async-done | bytes 2097168 | tf_op jit(solution)/shard_map/reduce_scatter | solution.py:527
  135.1 4.1 convert_element_type.88
  139.1 3.1 gather_fusion.3
  146.1 26.5 %all-gather.21.cloned.1.call-done.weight_ref = bf16[1024,2304]{1,0:T(8,128)(2,1)} async-done(((bf16[256,2304]{1,0:T(8,128)(2,1)}), bf16[1024,2304]{1,0:T(8,128)(2,1)}) %all-gather.21.cloned.1.call-update) | async-done | bytes 4718608 | tf_op jit(solution)/shard_map/all_gather | solution.py:532
  174.9 26.5 %mix_forward.1 = (f32[1024,2304]{1,0:T(8,128)}, f32[64,2048]{1,0:T(8,128)S(1)}, f32[64,1024]{1,0:T(8,128)S(1)}, f32[1024,128]{1,0:T(8,128)S(1)}, f32[64,128]{1,0...) custom-call(bf16[1024,1024]{1,0:T(8,128)(2,1)S(1)} %multiply_convert_fusion.2.normed_ref, ...), custom_call_target="tpu_custom_call" | custom-call | flops 9663676416 | bytes 16777216 | tf_op jit(solution)/shard_map/mix_forward/pallas_call | solution.py:212
  203.3 6.5 all-gather.23.cloned.1.call-done
  209.8 4.8 multiply_reduce_fusion.14
  215.7 29.9 %all-gather.25.cloned.1.call-done = bf16[2048,1024]{1,0:T(8,128)(2,1)} async-done(((bf16[512,1024]{1,0:T(8,128)(2,1)}), bf16[2048,1024]{1,0:T(8,128)(2,1)}) %all-gather.25.cloned.1.call-update) | async-done | bytes 4194320 | tf_op jit(solution)/shard_map/all_gather | solution.py:534
  245.7 3.4 multiply_reduce_fusion.19
  250.5 7.2 all_gather.80
  257.7 17.4 %fusion.59 = (f32[256]{0:T(256)S(1)}, f32[256,12672]{1,0:T(8,128)}) fusion(bf16[256,1024]{1,0:T(8,128)(2,1)S(1)} %all_gather.80, bf16[12672,1024]{1,0:T(8,128)(2,1)} %param.26), kind=kOutput, calls=%fused_computation.190 | convolution fusion | flops 6647021568 | bytes 39453696 | tf_op jit(solution)/shard_map/dot_general | solution.py:55
  275.1 7.1 select_reduce_fusion.1
  282.2 5.1 all-gather.10
  287.9 5.1 all-gather.11
  293.5 5.1 all-gather.9
  301.9 7.5 all_gather.88
  309.4 17.4 %fusion.60 = (f32[256]{0:T(256)S(1)}, f32[256,12672]{1,0:T(8,128)}) fusion(bf16[256,1024]{1,0:T(8,128)(2,1)S(1)} %all_gather.88, bf16[12672,1024]{1,0:T(8,128)(2,1)} %param.26), kind=kOutput, calls=%fused_computation.191 | convolution fusion | flops 6647021568 | bytes 39453696 | tf_op jit(solution)/shard_map/dot_general | solution.py:55
  326.8 7.1 select_reduce_fusion
  333.9 5.1 all-gather.13
  339.5 5.1 all-gather.14
  345.1 5.1 all-gather.12
  354.3 17.8 %while.20 = (s32[]{:T(128)}, f32[256]{0:T(256)}, f32[256]{0:T(256)}, f32[256]{0:T(256)S(1)}, f32[256]{0:T(256)}, /*index=5*/f32[256]{0:T(256)}, f32[256]{0:T(256...) while((s32[]{:T(128)}, f32[256]{0:T(256)}, ...), condition=%wide.region_12.13_spmd, body=%wide.region_11.12_spmd.sunk | while | flops 3586 | bytes 30873 | solution.py:38
  374.0 19.8 %fusion.53 = f32[256,1024]{1,0:T(8,128)} fusion(bf16[12672,1024]{1,0:T(8,128)(2,1)} %param.26, f32[256,12672]{1,0:T(8,128)} %get-tuple-element.320, f32[256]{0:T(256)S(1)} %get-tuple-element.277, s32[256]{0:T(256)} %sub.140), kind=kOutput, calls=%fused_computation.187 | convolution fusion | flops 6663241728 | bytes 39979008 | tf_op jit(solution)/shard_map/dot_general | solution.py:55
  396.1 20.3 %fusion.51 = f32[256,1024]{1,0:T(8,128)} fusion(bf16[12672,1024]{1,0:T(8,128)(2,1)} %param.26, f32[256,12672]{1,0:T(8,128)} %get-tuple-element.318, f32[256]{0:T(256)S(1)} %get-tuple-element.279, s32[256]{0:T(256)} %copy-done.34), kind=kOutput, calls=%fused_computation.185 | convolution fusion | flops 6663241728 | bytes 39979008 | tf_op jit(solution)/shard_map/dot_general | solution.py:55
  418.7 3.8 fusion.29
  422.5 24.1 %reduce-scatter.15.cloned.1.call-done = f32[64,1024]{1,0:T(8,128)} async-done(((f32[256,1024]{1,0:T(8,128)}), f32[64,1024]{1,0:T(8,128)}) %reduce-scatter.15.cloned.1.call-update) | async-done | bytes 262160 | tf_op jit(solution)/shard_map/reduce_scatter | solution.py:586
  446.6 3.1 multiply_reduce_fusion.15
  452.1 6.5 fusion.25
  458.7 4.8 multiply_reduce_fusion.12
  465.1 45.4 %mix_backward.1 = (bf16[1024,2304]{1,0:T(8,128)(2,1)}, f32[5,2304]{1,0:T(8,128)S(1)}, f32[32,1024]{1,0:T(8,128)S(1)}, f32[32,128]{1,0:T(8,128)S(1)}) custom-call(f32[1024,2304]{1,0:T(8,128)} %get-tuple-element.108.input_ref, f32[5,2304]{1,0:T(8,128)S(1)} %bitcast.150, f32[64,2048]{1,0:T(8,128)S(1)} %get-tuple-element.290.grad_ref, f32[64,1024]{1,0:T(8,128)S(1)} %copy-done.2, ...), custom_call_target="tpu_custom_call" | custom-call | flops 3221225472 | bytes 20971520 | tf_op jit(solution)/shard_map/mix_backward/pallas_call | solution.py:409
  513.3 5.2 fusion.62
  518.5 6.7 pad_maximum_fusion
  526.1 3.7 multiply_reduce_fusion.16
  529.9 9.0 fusion.61
  541.0 4.3 fusion.7
  546.9 21.5 %reduce-scatter.21.cloned.1.call-done = f32[512,1024]{1,0:T(8,128)} async-done(((f32[2048,1024]{1,0:T(8,128)}), f32[512,1024]{1,0:T(8,128)}) %reduce-scatter.21.cloned.1.call-update) | async-done | bytes 2097168 | tf_op jit(solution)/shard_map/reduce_scatter | solution.py:633
  568.3 137.1 %reduce-scatter.19.cloned.1.call-done = f32[256,4384]{1,0:T(8,128)} async-done(((f32[1024,4384]{1,0:T(8,128)}), f32[256,4384]{1,0:T(8,128)}) %reduce-scatter.19.cloned.1.call-update) | async-done | bytes 4489232 | tf_op jit(solution)/shard_map/reduce_scatter | solution.py:632
  705.6 27.7 %fusion.52 = f32[12672,1024]{1,0:T(8,128)} fusion(bf16[256,1024]{1,0:T(8,128)(2,1)S(1)} %copy-done.19, f32[256,12672]{1,0:T(8,128)} %get-tuple-element.318, f32[256]{0:T(256)S(1)} %copy-done.44, s32[256]{0:T(256)S(1)} %copy-done.35), kind=kOutput, calls=%fused_computation.186 | convolution fusion | flops 6663241728 | bytes 65406976 | tf_op jit(solution)/shard_map/dot_general | solution.py:55
  733.3 38.9 %convolution_add_fusion = f32[12672,1024]{1,0:T(8,128)} fusion(f32[12672,1024]{1,0:T(8,128)} %fusion.52, bf16[256,1024]{1,0:T(8,128)(2,1)S(1)} %copy-done.21, f32[256,12672]{1,0:T(8,128)} %get-tuple-element.320, f32[256]{0:T(256)S(1)} %copy-done.50, s32[256]{0:T(256)S(1)} %copy-done.42), kind=kOutput, calls=%fused_computation.13 | convolution fusion | flops 6676217856 | bytes 117311488 | tf_op jit(solution)/shard_map/dot_general | solution.py:55
  772.3 9.8 convert_select_fusion
  782.1 70.7 %scatter_fusion = f32[12672,1024]{1,0:T(8,128)} fusion(f32[12672,1024]{1,0:T(8,128)} %convolution_add_fusion, s32[4096]{0:T(1024)S(1)} %bitcast.159, f32[4096,1024]{1,0:T(8,128)} %convert_select_fusion), kind=kCustom, calls=%fused_computation.4 | custom fusion | flops 4194304 | bytes 50348032 | tf_op jit(solution)/shard_map/scatter-add | solution.py:640
  852.8 26.7 %convert_element_type.107 = bf16[12672,1024]{1,0:T(8,128)(2,1)} convert(f32[12672,1024]{1,0:T(8,128)} %scatter_fusion) | non-fusion elementwise | flops 12976128 | bytes 77856768 | tf_op jit(solution)/shard_map/convert_element_type | solution.py:642
  879.5 30.9 %copy.106 = bf16[12672,1024]{0,1:T(8,128)(2,1)} copy(bf16[12672,1024]{1,0:T(8,128)(2,1)} %convert_element_type.107) | data formatting | bytes 51904512
  917.4 3.7 fusion.2
  927.5 10.9 all-reduce.5
  939.6 111.4 %all-reduce.9.cloned.1.call-done = (f32[256,4384]{1,0:T(8,128)}, f32[512,1024]{1,0:T(8,128)}, f32[256,1024]{1,0:T(8,128)}) async-done(((f32[256,4384]{1,0:T(8,128)}, f32[512,1024]{1,0:T(8,128)}, f32[256,1024]{1,0:T(8,128)}), (f32[256,4384]{1,0:T(8,128)}, f32[512,1024]{1,0:T(8,128)}, f32[256,1024]{1,0:T(8,128)})) %all-reduce.9.cloned.1.call-update) | async-done | bytes 7634960 | tf_op jit(solution)/shard_map/psum | solution.py:644
  1055.9 4.6 multiply_reduce_fusion.4
  1060.5 408.0 %reduce-scatter.25.cloned.1.call-done = bf16[128,12672]{1,0:T(8,128)(2,1)} async-done(((bf16[1024,12672]{1,0:T(8,128)(2,1)}), bf16[128,12672]{1,0:T(8,128)(2,1)}) %reduce-scatter.25.cloned.1.call-update) | async-done | bytes 3244048
  1468.5 4.7 copy.107
  1475.7 36.1 %all-reduce.10 = (f32[12672]{0:T(1024)S(1)}, f32[5,576]{1,0:T(8,128)S(1)}, f32[3,8]{0,1:T(8,128)S(1)}, f32[1024]{0:T(1024)S(1)}, f32[1]{0:T(128)}, /*index=5*/f32[]{:T(128)}) all-reduce(f32[12672]{0:T(1024)S(1)} %get-tuple-element.210, f32[5,576]{1,0:T(8,128)S(1)} %copy.109, ...), channel_id=1, replica_groups=mesh['dp'=8,'fsdp'=4] {'dp'}, use_global_device_ids=true, to_apply=%region_22.23 | all-reduce | flops 16602 | bytes 132816 | tf_op jit(solution)/shard_map/psum | solution.py:670
  1514.2 11.5 stack.75
  1525.8 11.3 all-reduce.4
  1550.6 6.4 convert_subtract_fusion.1
  1557.0 5.9 copy.102
  1568.2 3.8 convert_subtract_fusion.2
  1572.1 8.5 convert_subtract_fusion
  (341 shorter events, 99.0 us)
Async XLA Ops:
  7.2 125.8 %reduce-scatter.13.cloned.1.call-start = ((), (), s32[]{:S(2)}) async-start(), calls=%async_computation.8 | async-start | bytes 10485760 | tf_op jit(solution)/shard_map/reduce_scatter | solution.py:527
  19.5 32.7 %copy-start.38 = (pred[1,8,4,128]{3,1,2,0:T(8,128)(4,1)}, pred[1,8,4,128]{3,1,2,0:T(8,128)(4,1)S(1)}, u32[]{:S(2)}) copy-start(pred[1,8,4,128]{3,1,2,0:T(8,128)(4,1)S(1)} %copy.129) | copy-start | bytes 12292
  19.5 32.6 %copy-start.27 = (s32[4096,1]{0,1:T(1,128)}, s32[4096,1]{0,1:T(1,128)S(1)}, u32[]{:S(2)}) copy-start(s32[4096,1]{0,1:T(1,128)S(1)} %compare_select_fusion) | copy-start | bytes 49156
  59.4 7.8 copy-start.47
  59.4 13.3 copy-start.69
  59.4 19.3 %copy-start.29 = (bf16[5,576]{1,0:T(8,128)(2,1)S(1)}, bf16[5,576]{1,0:T(8,128)(2,1)}, u32[]{:S(2)}) copy-start(bf16[5,576]{1,0:T(8,128)(2,1)} %param.30) | copy-start | bytes 17284
  59.4 24.6 %slice-start = ((bf16[256,4384]{0,1:T(8,128)(2,1)}), bf16[256,32]{0,1:T(8,128)(2,1)S(1)}, s32[]{:S(2)}) async-start(bf16[256,4384]{0,1:T(8,128)(2,1)} %param.27), calls=%async_computation.22 | async-start | bytes 32768 | tf_op jit(solution)/shard_map/slice | solution.py:533
  59.5 113.1 %all-gather.21.cloned.1.call-start = ((), (), s32[]{:S(2)}) async-start(), calls=%async_computation.9 | async-start | bytes 5898240 | tf_op jit(solution)/shard_map/all_gather | solution.py:532
  62.5 15.3 copy-start.8
  63.7 146.2 %all-gather.23.cloned.1.call-start = ((), (), s32[]{:S(2)}) async-start(), calls=%async_computation.10 | async-start | bytes 5242880 | tf_op jit(solution)/shard_map/all_gather | solution.py:531
  66.0 179.6 %all-gather.25.cloned.1.call-start = ((), (), s32[]{:S(2)}) async-start(), calls=%async_computation.11 | async-start | bytes 5242880 | tf_op jit(solution)/shard_map/all_gather | solution.py:534
  66.6 233.1 %all-gather.27.cloned.1.call-start = ((), (), s32[]{:S(2)}) async-start(), calls=%async_computation.12 | async-start | bytes 2621440 | tf_op jit(solution)/shard_map/all_gather | solution.py:535
  67.2 351.5 %reduce-scatter.17.cloned.1.call-start = ((), (), s32[]{:S(2)}) async-start(), calls=%async_computation.14 | async-start | bytes 1310720 | tf_op jit(solution)/shard_map/reduce_scatter | solution.py:587
  78.7 196.4 %copy-start.34 = (s32[256]{0:T(256)}, s32[256]{0:T(256)S(1)}, u32[]{:S(2)}) copy-start(s32[256]{0:T(256)S(1)} %sub.136) | copy-start | bytes 3076
  89.9 55.5 %copy-start.23 = (bf16[1024,32]{0,1:T(8,128)(2,1)}, bf16[1024,32]{0,1:T(8,128)(2,1)S(1)}, u32[]{:S(2)}) copy-start(bf16[1024,32]{0,1:T(8,128)(2,1)S(1)} %all_gather.76) | copy-start | bytes 196612
  135.0 7.9 copy-start.36
  135.1 7.9 copy-start.32
  257.7 17.4 %copy-start.18 = (bf16[256,1024]{1,0:T(8,128)(2,1)}, bf16[256,1024]{1,0:T(8,128)(2,1)S(1)}, u32[]{:S(2)}) copy-start(bf16[256,1024]{1,0:T(8,128)(2,1)S(1)} %all_gather.80) | copy-start | bytes 1572868
  309.4 17.4 %copy-start.20 = (bf16[256,1024]{1,0:T(8,128)(2,1)}, bf16[256,1024]{1,0:T(8,128)(2,1)S(1)}, u32[]{:S(2)}) copy-start(bf16[256,1024]{1,0:T(8,128)(2,1)S(1)} %all_gather.88) | copy-start | bytes 1572868
  309.4 17.4 %copy-start.41 = (s32[256]{0:T(256)S(1)}, s32[256]{0:T(256)}, u32[]{:S(2)}) copy-start(s32[256]{0:T(256)} %sub.140) | copy-start | bytes 3076
  326.7 24.0 %slice-start.1 = ((f32[4,1,256]{2,1,0:T(1,128)}), f32[3,1,256]{2,1,0:T(1,128)S(1)}, s32[]{:S(2)}) async-start(f32[4,1,256]{2,1,0:T(1,128)} %copy-done.55), calls=%async_computation.23 | async-start | bytes 6144 | tf_op jit(solution)/shard_map/slice | solution.py:37
  326.7 24.6 %copy-start.59 = (f32[3,1,256]{2,1,0:T(1,128)S(1)}, f32[3,1,256]{2,1,0:T(1,128)}, u32[]{:S(2)}) copy-start(f32[3,1,256]{2,1,0:T(1,128)} %slice.213) | copy-start | bytes 9220
  326.7 25.2 %copy-start.60 = (f32[3,1,256]{2,1,0:T(1,128)S(1)}, f32[3,1,256]{2,1,0:T(1,128)}, u32[]{:S(2)}) copy-start(f32[3,1,256]{2,1,0:T(1,128)} %slice.211) | copy-start | bytes 9220
  393.8 52.8 %reduce-scatter.15.cloned.1.call-start = ((), (), s32[]{:S(2)}) async-start(), calls=%async_computation.13 | async-start | bytes 1310720 | tf_op jit(solution)/shard_map/reduce_scatter | solution.py:586
  416.4 35.7 %copy-start.57 = (f32[64]{0:T(128)S(1)}, f32[64]{0:T(128)}, u32[]{:S(2)}) copy-start(f32[64]{0:T(128)} %fusion.47) | copy-start | bytes 772
  416.4 130.4 %reduce-scatter.23.cloned.1.call-start = ((), (), s32[]{:S(2)}) async-start(), calls=%async_computation.18 | async-start | bytes 5242880 | tf_op jit(solution)/shard_map/reduce_scatter | solution.py:634
  422.5 145.9 %reduce-scatter.21.cloned.1.call-start = ((), (), s32[]{:S(2)}) async-start(), calls=%async_computation.17 | async-start | bytes 10485760 | tf_op jit(solution)/shard_map/reduce_scatter | solution.py:633
  458.6 246.9 %reduce-scatter.19.cloned.1.call-start = ((), (), s32[]{:S(2)}) async-start(), calls=%async_computation.16 | async-start | bytes 22937600 | tf_op jit(solution)/shard_map/reduce_scatter | solution.py:632
  465.1 46.2 %copy-start.16 = (bf16[64,2048]{1,0:T(8,128)(2,1)}, bf16[64,2048]{1,0:T(8,128)(2,1)S(1)}, u32[]{:S(2)}) copy-start(bf16[64,2048]{1,0:T(8,128)(2,1)S(1)} %get-tuple-element.289) | copy-start | bytes 786436
  465.1 46.2 %copy-start.11 = (f32[64,1024]{1,0:T(8,128)S(1)}, f32[64,1024]{1,0:T(8,128)}, u32[]{:S(2)}) copy-start(f32[64,1024]{1,0:T(8,128)} %copy-done.10) | copy-start | bytes 786436
  465.1 46.2 %copy-start.58 = (f32[64]{0:T(128)S(1)}, f32[64]{0:T(128)}, u32[]{:S(2)}) copy-start(f32[64]{0:T(128)} %fusion.46) | copy-start | bytes 772
  525.2 247.1 %all-gather.29.cloned.1.call-start = ((), (), s32[]{:S(2)}) async-start(), calls=%async_computation.15 | async-start | bytes 10485760 | tf_op jit(solution)/shard_map/all_gather | solution.py:626
  529.8 9.0 copy-start.7
  529.8 9.0 copy-start.24
  529.9 9.0 copy-start.33
  545.3 160.3 %copy-start.19 = (bf16[256,1024]{1,0:T(8,128)(2,1)S(1)}, bf16[256,1024]{1,0:T(8,128)(2,1)}, u32[]{:S(2)}) copy-start(bf16[256,1024]{1,0:T(8,128)(2,1)} %copy-done.18) | copy-start | bytes 1572868
  545.3 160.3 %copy-start.35 = (s32[256]{0:T(256)S(1)}, s32[256]{0:T(256)}, u32[]{:S(2)}) copy-start(s32[256]{0:T(256)} %copy-done.34) | copy-start | bytes 3076
  545.3 160.3 %copy-start.44 = (f32[256]{0:T(256)S(1)}, f32[256]{0:T(256)}, u32[]{:S(2)}) copy-start(f32[256]{0:T(256)} %copy-done.43) | copy-start | bytes 3076
  545.3 393.2 %reduce-scatter.27.cloned.1.call-start = ((), (), s32[]{:S(2)}) async-start(), calls=%async_computation.20 | async-start | bytes 1474560
  546.8 504.2 %all-reduce.9.cloned.1.call-start = ((), (), s32[]{:S(2)}) async-start(), calls=%async_computation.21 | async-start | bytes 15466496 | tf_op jit(solution)/shard_map/psum | solution.py:644
  705.5 27.8 %copy-start.21 = (bf16[256,1024]{1,0:T(8,128)(2,1)S(1)}, bf16[256,1024]{1,0:T(8,128)(2,1)}, u32[]{:S(2)}) copy-start(bf16[256,1024]{1,0:T(8,128)(2,1)} %copy-done.20) | copy-start | bytes 1572868
  705.5 27.8 %copy-start.42 = (s32[256]{0:T(256)S(1)}, s32[256]{0:T(256)}, u32[]{:S(2)}) copy-start(s32[256]{0:T(256)} %sub.140) | copy-start | bytes 3076
  705.5 27.8 %copy-start.50 = (f32[256]{0:T(256)S(1)}, f32[256]{0:T(256)}, u32[]{:S(2)}) copy-start(f32[256]{0:T(256)} %copy-done.49) | copy-start | bytes 3076
  705.5 763.0 %reduce-scatter.25.cloned.1.call-start = ((), (), s32[]{:S(2)}) async-start(), calls=%async_computation.19 | async-start | bytes 29196288
  733.3 38.9 %copy-start.39 = (pred[1,8,4,128]{3,1,2,0:T(8,128)(4,1)S(1)}, pred[1,8,4,128]{3,1,2,0:T(8,128)(4,1)}, u32[]{:S(2)}) copy-start(pred[1,8,4,128]{3,1,2,0:T(8,128)(4,1)} %copy-done.38) | copy-start | bytes 12292
  772.3 9.8 copy-start.28
  910.4 10.7 copy-start.12
  910.5 13.9 copy-start.9
  910.5 16.9 %copy-start.51 = (f32[1024]{0:T(1024)S(1)}, f32[1024]{0:T(1024)}, u32[]{:S(2)}) copy-start(f32[1024]{0:T(1024)} %get-tuple-element.204) | copy-start | bytes 12292
  910.5 16.9 %copy-start.56 = (f32[1024]{0:T(1024)S(1)}, f32[1024]{0:T(1024)}, u32[]{:S(2)}) copy-start(f32[1024]{0:T(1024)} %get-tuple-element.219) | copy-start | bytes 12292
  910.5 17.0 %copy-start.40 = (f32[2048]{0:T(1024)S(1)}, f32[2048]{0:T(1024)}, u32[]{:S(2)}) copy-start(f32[2048]{0:T(1024)} %get-tuple-element.217) | copy-start | bytes 24580
  910.5 17.0 %copy-start.54 = (f32[1024]{0:T(1024)S(1)}, f32[1024]{0:T(1024)}, u32[]{:S(2)}) copy-start(f32[1024]{0:T(1024)} %get-tuple-element.221) | copy-start | bytes 12292
  1055.9 494.6 %copy-start.45 = (f32[4384]{0:T(1024)S(1)}, f32[4384]{0:T(1024)}, u32[]{:S(2)}) copy-start(f32[4384]{0:T(1024)} %param.36) | copy-start | bytes 52612
  1539.1 33.0 %copy-start.25 = (f32[12672]{0:T(1024)}, f32[12672]{0:T(1024)S(1)}, u32[]{:S(2)}) copy-start(f32[12672]{0:T(1024)S(1)} %multiply_add_fusion.2) | copy-start | bytes 152068
  1539.8 25.8 %copy-start.64 = (f32[256]{0:T(256)}, f32[256]{0:T(256)S(1)}, u32[]{:S(2)}) copy-start(f32[256]{0:T(256)S(1)} %multiply_add_fusion.8) | copy-start | bytes 3076
  1539.8 28.4 %copy-start.61 = (f32[512]{0:T(512)}, f32[512]{0:T(512)S(1)}, u32[]{:S(2)}) copy-start(f32[512]{0:T(512)S(1)} %multiply_add_fusion.7) | copy-start | bytes 6148
  1540.5 22.4 %copy-start.65 = (f32[256]{0:T(256)}, f32[256]{0:T(256)S(1)}, u32[]{:S(2)}) copy-start(f32[256]{0:T(256)S(1)} %multiply_add_fusion.9) | copy-start | bytes 3076
  1550.6 12.3 copy-start.31
  1557.0 7.3 copy-start.67
  1557.0 7.4 copy-start.68
  1557.0 8.0 copy-start.46
  1564.2 16.3 %copy-start.75 = (f32[128]{0:T(128)}, f32[128]{0:T(128)S(1)}, u32[]{:S(2)}) copy-start(f32[128]{0:T(128)S(1)} %multiply_add_fusion.10) | copy-start | bytes 1540
  1564.3 16.3 %copy-start.52 = (f32[1024]{0:T(1024)}, f32[1024]{0:T(1024)S(1)}, u32[]{:S(2)}) copy-start(f32[1024]{0:T(1024)S(1)} %multiply_add_fusion.5) | copy-start | bytes 12292
  1564.3 16.3 %copy-start.53 = (f32[1024]{0:T(1024)}, f32[1024]{0:T(1024)S(1)}, u32[]{:S(2)}) copy-start(f32[1024]{0:T(1024)S(1)} %multiply_add_fusion.4) | copy-start | bytes 12292
  (38 other events, 101.2 us)
Sparse Core Ops, SparseCore 0:
  59.5 73.3 reduce-scatter.12
  135.1 37.4 all-gather.20
  174.7 35.0 all-gather.22
  211.3 34.3 all-gather.24
  247.1 22.5 all-gather.26
  393.9 24.7 reduce-scatter.16
  421.8 24.7 reduce-scatter.14
  449.7 44.5 reduce-scatter.22
  496.9 71.3 reduce-scatter.20
  570.8 134.6 reduce-scatter.18
  707.6 58.2 all-gather.28
  768.9 25.6 reduce-scatter.26
  799.0 251.9 all-reduce.8
  1054.8 413.7 reduce-scatter.24

commit v2 on v1

--- a/solution.py
+++ b/solution.py
@@ -19,6 +19,11 @@
 GROUP = 4
 PAD = 8
 CHUNK = 128
+ROW_CHUNK = 512
+TABLE_BLOCKS = 11
+UNROLL = 8
+ID_BITS = 14
+TOK_DEV = 1024
 
 
 PRECISE = lax.Precision.HIGHEST
@@ -458,6 +463,147 @@
     )(inputs, taps, grad, scores, keys, queries, steps, decay, raw, columns, places, skip)
 
 
+def table_kernel(
+    first_id_ref,
+    table_ref,
+    rows_ref,
+    columns_ref,
+    marks_ref,
+    own_ref,
+    other_ref,
+):
+    block = table_ref.shape[0]
+    width = own_ref.shape[1]
+    count = rows_ref.shape[0] // ROW_CHUNK
+    entries = (
+        first_id_ref[0]
+        + pl.program_id(0) * block
+        + lax.broadcasted_iota(jnp.int32, (block, ROW_CHUNK), 0)
+    )
+    table = table_ref[...]
+
+    def part(start):
+        logits = product(table, rows_ref[pl.ds(start, ROW_CHUNK), :], 1, 1)
+        marks = marks_ref[:, pl.ds(start, ROW_CHUNK)]
+        share = jnp.exp(logits - marks[0:1])
+        share = jnp.where(entries == marks[1:2].astype(jnp.int32), share - 1.0, share)
+        grad = (share * marks[2:3]).astype(jnp.bfloat16)
+        return product(grad, columns_ref[pl.ds(start, ROW_CHUNK), :], 1, 0)
+
+    def body(index, total):
+        start = pl.multiple_of(index * 2 * ROW_CHUNK, 2 * ROW_CHUNK)
+        return total + (part(start) + part(start + ROW_CHUNK))
+
+    total = lax.fori_loop(0, count // 2, body, jnp.zeros((block, 2 * width), jnp.float32))
+    own_ref[...] = total[:, :width]
+    other_ref[...] = total[:, width:].astype(other_ref.dtype)
+
+
+def table_grads(first_id, table, rows, columns, marks):
+    vocab_part = table.shape[0]
+    width = columns.shape[1] // 2
+    block = vocab_part // TABLE_BLOCKS
+    once = lambda shape: pl.BlockSpec(
+        shape, lambda step: (0,) * len(shape), pipeline_mode=pl.Buffered(1)
+    )
+    return pl.pallas_call(
+        table_kernel,
+        grid=(TABLE_BLOCKS,),
+        in_specs=[
+            pl.BlockSpec(memory_space=pltpu.SMEM),
+            pl.BlockSpec((block, D), lambda step: (step, 0)),
+            once(rows.shape),
+            once(columns.shape),
+            once(marks.shape),
+        ],
+        out_specs=[
+            pl.BlockSpec((block, width), lambda step: (step, 0)),
+            pl.BlockSpec((block, width), lambda step: (step, 0)),
+        ],
+        out_shape=[
+            jax.ShapeDtypeStruct((vocab_part, width), jnp.float32),
+            jax.ShapeDtypeStruct((vocab_part, width), jnp.bfloat16),
+        ],
+        compiler_params=pltpu.CompilerParams(vmem_limit_bytes=56 << 20),
+        cost_estimate=pl.CostEstimate(
+            flops=2 * vocab_part * rows.shape[0] * (D + 2 * width),
+            bytes_accessed=2 * vocab_part * D + 6 * vocab_part * width,
+            transcendentals=vocab_part * rows.shape[0],
+        ),
+        name="table_grads",
+    )(first_id, table, rows, columns, marks)
+
+
+def token_kernel(
+    counts_ref,
+    listing_ref,
+    grads_ref,
+    own_ref,
+    other_ref,
+    out_ref,
+    held,
+    second,
+    third,
+    fourth,
+):
+    step = pl.program_id(0)
+    length = grads_ref.shape[1]
+    totals = (out_ref, second, third, fourth)
+
+    @pl.when(step == 0)
+    def _():
+        out_ref[...] = own_ref[...] + other_ref[...].astype(jnp.float32)
+        for total in totals[1:]:
+            total[...] = jnp.zeros_like(total)
+        held[length:, :] = jnp.zeros((PAD, held.shape[1]), jnp.float32)
+
+    held[0:length, :] = grads_ref[0].astype(jnp.float32)
+
+    def body(index, carry):
+        for offset in range(UNROLL):
+            entry = listing_ref[0, 0, index * UNROLL + offset]
+            source = lax.shift_right_logical(entry, ID_BITS) & (2 * TOK_DEV - 1)
+            target = entry & ((1 << ID_BITS) - 1)
+            total = totals[offset % len(totals)]
+            total[pl.ds(target, 1), :] += held[pl.ds(source, 1), :]
+        return carry
+
+    lax.fori_loop(0, (counts_ref[step] + UNROLL - 1) // UNROLL, body, 0)
+
+    @pl.when(step == pl.num_programs(0) - 1)
+    def _():
+        out_ref[...] += second[...] + (third[...] + fourth[...])
+
+
+def token_grads(counts, listing, grads, own, other):
+    sources, length, width = grads.shape
+    once = lambda shape: pl.BlockSpec(
+        shape, lambda step: (0,) * len(shape), pipeline_mode=pl.Buffered(1)
+    )
+    return pl.pallas_call(
+        token_kernel,
+        grid=(sources,),
+        in_specs=[
+            pl.BlockSpec(memory_space=pltpu.SMEM),
+            pl.BlockSpec((1, 1, length), lambda step: (step, 0, 0), memory_space=pltpu.SMEM),
+            pl.BlockSpec((1, length, width), lambda step: (step, 0, 0)),
+            once(own.shape),
+            once(other.shape),
+        ],
+        out_specs=pl.BlockSpec(own.shape, lambda step: (0, 0)),
+        out_shape=jax.ShapeDtypeStruct(own.shape, jnp.float32),
+        scratch_shapes=[pltpu.VMEM((length + PAD, width), jnp.float32)]
+        + [pltpu.VMEM(own.shape, jnp.float32)] * 3,
+        compiler_params=pltpu.CompilerParams(vmem_limit_bytes=56 << 20),
+        cost_estimate=pl.CostEstimate(
+            flops=sources * length * width,
+            bytes_accessed=64 << 20,
+            transcendentals=0,
+        ),
+        name="token_grads",
+    )(counts, listing, grads, own, other)
+
+
 def shard_terms(logits, local_target):
     row_max = jnp.max(logits, axis=1)
     exp_total = jnp.sum(jnp.exp(logits - row_max[:, None]), axis=1)
@@ -521,6 +667,17 @@
     local_ids = all_tokens - first_id
     inside = (local_ids >= 0) & (local_ids < vocab_part)
     safe_ids = jnp.clip(local_ids, 0, vocab_part - 1)
+    every_token = lax.all_gather(tokens, ("fsdp", "dp"), axis=0)
+    every_id = every_token - first_id
+    every_inside = (every_id >= 0) & (every_id < vocab_part)
+    slot = jnp.arange(seq_len, dtype=jnp.int32)[None, :]
+    listing = lax.sort(
+        jnp.where(every_inside, (slot << ID_BITS) + every_id, (2 * seq_len - 1) * (1 << ID_BITS)),
+        dimension=1,
+        is_stable=False,
+    )
+    listing = jnp.where(listing < (seq_len << ID_BITS), listing, seq_len << ID_BITS)
+    inside_counts = jnp.sum(every_inside.astype(jnp.int32), axis=1)
     looked = jnp.where(inside[:, None], embedding[safe_ids], jnp.zeros((), jnp.bfloat16)).astype(
         jnp.float32
     )
@@ -622,31 +779,75 @@
         jnp.float32
     )
     d_embedded = d_pre + jnp.dot(onehot, d_residual + d_pre_rows, precision=PRECISE)
-    d_in_weight = jnp.concatenate([d_in_gate, d_in_conv, d_in_step], axis=1)
-    group_grads = lax.all_gather(
-        d_embedded.astype(jnp.bfloat16), "fsdp", axis=0, tiled=True
-    ).astype(d_embedded.dtype)
-    masked_grads = jnp.where(inside[:, None], group_grads, 0.0)
     d_gains = jnp.concatenate([d_gain_first, d_gain_final, d_gain_mix])
+    low_shares = tuple(
+        lax.psum_scatter(gradient.astype(jnp.bfloat16), "fsdp", scatter_dimension=0, tiled=True)
+        for gradient in (d_in_conv, d_in_gate, d_out_weight, d_ahead)
+    )
     shares = (
-        lax.psum_scatter(d_in_weight, "fsdp", scatter_dimension=0, tiled=True),
-        lax.psum_scatter(d_out_weight, "fsdp", scatter_dimension=0, tiled=True),
-        lax.psum_scatter(d_ahead, "fsdp", scatter_dimension=0, tiled=True),
+        lax.psum_scatter(d_in_step, "fsdp", scatter_dimension=0, tiled=True),
         lax.psum_scatter(d_conv, "fsdp", scatter_dimension=1, tiled=True),
         lax.psum_scatter(d_heads, "fsdp", scatter_dimension=1, tiled=True),
         lax.psum_scatter(d_gains, "fsdp", scatter_dimension=0, tiled=True),
     )
-    d_table = contract(grad_next, group_first, 0, 0) + contract(grad_after, group_second, 0, 0)
-    d_table = d_table.at[safe_ids].add(masked_grads)
-    table_own = lax.psum_scatter(
-        d_table.astype(jnp.bfloat16), "dp", scatter_dimension=1, tiled=True
+    column_start = replica_rank * column_part
+    other_start = (replica_rank ^ 1) * column_part
+    peers = [list(range(parity, replica_count, 2)) for parity in range(2)]
+    pair_rows = lax.all_gather(
+        jnp.concatenate([group_first, group_second]), "dp", axis=0, tiled=True, axis_index_groups=peers
+    )
+    pair_marks = lax.all_gather(
+        jnp.stack(
+            [
+                jnp.concatenate([lse_next, lse_after]),
+                jnp.concatenate([next_ids, after_ids]).astype(jnp.float32),
+            ]
+        ),
+        "dp",
+        axis=1,
+        tiled=True,
+        axis_index_groups=peers,
+    )
+    row_shares = jnp.where(
+        jnp.arange(pair_rows.shape[0]) % (2 * group_size * loss_rows) < group_size * loss_rows,
+        1.0 / count_all,
+        AFTER_SHARE / count_all,
     ).astype(jnp.float32)
-    summed = lax.psum(
-        (shares[0], shares[1], shares[2], shares[3], shares[4], shares[5], group_loss), "dp"
-    )
-    gradients = [table_own] + list(summed[:6])
-    loss = summed[6]
-    column_start = replica_rank * column_part
+    own_table, other_table = table_grads(
+        jnp.reshape(first_id, (1,)).astype(jnp.int32),
+        embedding,
+        pair_rows,
+        jnp.concatenate(
+            [
+                lax.dynamic_slice_in_dim(pair_rows, column_start, column_part, 1),
+                lax.dynamic_slice_in_dim(pair_rows, other_start, column_part, 1),
+            ],
+            axis=1,
+        ),
+        jnp.concatenate([pair_marks, row_shares[None, :]]),
+    )
+    other_table = lax.ppermute(
+        other_table, "dp", [(index, index ^ 1) for index in range(replica_count)]
+    )
+    column_grads = lax.all_to_all(
+        d_embedded.astype(jnp.bfloat16).reshape(seq_len, replica_count, column_part),
+        "dp",
+        split_axis=1,
+        concat_axis=0,
+    )
+    column_grads = lax.all_gather(column_grads, "fsdp", axis=0, tiled=True)
+    table_own = token_grads(
+        inside_counts, listing[:, None, :], column_grads, own_table, other_table
+    )
+    low_sums = [total.astype(jnp.float32) for total in lax.psum(low_shares, "dp")]
+    sums = lax.psum((shares, group_loss), "dp")
+    loss = sums[1]
+    gradients = [
+        table_own,
+        jnp.concatenate([low_sums[1], low_sums[0], sums[0][0]], axis=1),
+        low_sums[2],
+        low_sums[3],
+    ] + list(sums[0][1:])
     table_old = lax.dynamic_slice_in_dim(embedding, column_start, column_part, 1).astype(
         jnp.float32
     )

time: 1600 us -> 1200 us (0.75)
  waiting for transfers between devices: 812 us -> 250 us
  blocking collectives: 131 us -> 327 us
  Pallas kernels: 71.9 us -> 210 us
  other arithmetic: 216 us -> 119 us
  matrix products: 197 us -> 136 us
  local copies, waits for them, and re-layouts: 130 us -> 114 us
    unnamed x16 -> x17, waiting for transfers between devices: 409 us -> 1.29 us
    reduce_scatter x3 -> x5, waiting for transfers between devices: 159 us -> 12 us  [the longest x4 12 us: shards(): lax.psum_scatter(gradient.astype(jnp.bfloat16), 'fsdp', scatter_dimension...]
    pallas_call x0 -> x2, Pallas kernels: none -> 138 us  [the longest x1 103 us: table_grads(): pl.pallas_call(table_kernel, grid=(TABLE_BLOCKS,), in_specs=[pl.BlockSpec...]
    all_to_all x0 -> x1, blocking collectives: none -> 106 us  [shards(): lax.all_to_all(d_embedded.astype(jnp.bfloat16).reshape(seq_len, replica_c...]
    all_gather x0 -> x2, blocking collectives: none -> 81 us  [the longest x1 67.7 us: shards(): every_token = lax.all_gather(tokens, ('fsdp', 'dp'), axis=0)]
    psum x1, waiting for transfers between devices: 111 us -> 40.3 us  [shards(): lax.psum(low_shares, 'dp')]
    scatter-add x1 -> x0, other arithmetic: 70.7 us -> none  [shards(): d_table = d_table.at[safe_ids].add(masked_grads)]
    dot_general x19 -> x17, matrix products: 190 us -> 128 us  [contract(): lax.dot_general(one_side, other_side, (((one_dim,), (other_dim,)), ((), (...]
  transfers between devices with their start and end apart: 14 -> 17, of which waited for: 10 -> 11; matrix products, arithmetic and copies ran while one was open for 23% -> 13% of each run, Pallas kernels for 5% -> 18%
where the time goes in v2:
time: 1200 us; the launch traced here: 1190 us
  blocking collectives  327 us (27%)
  waiting for transfers between devices  250 us (21%)
  Pallas kernels  210 us (18%)
  matrix products  136 us (11%)
  other arithmetic  119 us (10%)
  local copies, waits for them, and re-layouts  114 us (10%)
  between operations  31.8 us (3%)
    dot_general x17, matrix products, contract(): lax.dot_general(one_side, other_side, (((one_dim,), (other_dim,)), ((), (...  128 us
    all_to_all x1, blocking collectives, shards(): lax.all_to_all(d_embedded.astype(jnp.bfloat16).reshape(seq_len, replica_c...  106 us
    pallas_call x1, Pallas kernels, table_grads(): pl.pallas_call(table_kernel, grid=(TABLE_BLOCKS,), in_specs=[pl.BlockSpec...  103 us
    all_gather x1, blocking collectives, shards(): every_token = lax.all_gather(tokens, ('fsdp', 'dp'), axis=0)  67.7 us
    all_gather x1, waiting for transfers between devices, shards(): column_grads = lax.all_gather(column_grads, 'fsdp', axis=0, tiled=True)  45.6 us
    pallas_call x1, Pallas kernels, mix_backward(): pl.pallas_call(mix_backward_kernel, grid=(blocks,), in_specs=[pl.BlockSpe...  45.3 us
    psum x1, blocking collectives, shards(): lax.psum((jnp.sum(squares[0], axis=1), jnp.sum(table_old * table_old)), '...  40.4 us
    psum x1, waiting for transfers between devices, shards(): lax.psum(low_shares, 'dp')  40.3 us
  transfers between devices with their start and end apart: 17, of which 11 were waited for; matrix products, arithmetic and copies ran while one was open for 13% of the time, Pallas kernels for 18%

profile of v2, /device:TPU:0, one launch (start us, length us, event | category | flops | bytes accessed | tf_op | source)
XLA Modules:
  0.0 1191.0 jit_solution(1244034632795916185)
XLA Ops:
  14.0 6.3 all-gather.8
  20.4 32.6 %gather_fusion.2 = bf16[4096,1024]{1,0:T(8,128)(2,1)} fusion(bf16[12672,1024]{1,0:T(8,128)(2,1)} %table_ref.1, s32[4096]{0:T(1024)S(1)} %broadcast_clamp_fusion), kind=kCustom, calls=%fused_computation.2 | custom fusion | bytes 16793600 | tf_op jit(solution)/shard_map/gather | solution.py:681
  53.0 7.2 broadcast_select_fusion
  60.3 4.2 copy.129
  70.6 5.4 all_gather.87
  76.6 5.3 all_gather.90
  81.9 5.1 all-gather.10
  87.1 5.7 all-gather.9
  94.3 39.3 %reduce-scatter.12.cloned.1.call-done = bf16[1024,1024]{1,0:T(8,128)(2,1)} async-done(((bf16[4096,1024]{1,0:T(8,128)(2,1)}), bf16[1024,1024]{1,0:T(8,128)(2,1)}) %reduce-scatter.12.cloned.1.call-update) | async-done | bytes 2097168 | tf_op jit(solution)/shard_map/reduce_scatter | solution.py:684
  136.3 4.1 convert_element_type.117
  140.4 3.3 gather_fusion.3
  147.7 25.5 %all-gather.24.cloned.1.call-done.weight_ref = bf16[1024,2304]{1,0:T(8,128)(2,1)} async-done(((bf16[256,2304]{1,0:T(8,128)(2,1)}), bf16[1024,2304]{1,0:T(8,128)(2,1)}) %all-gather.24.cloned.1.call-update) | async-done | bytes 4718608 | tf_op jit(solution)/shard_map/all_gather | solution.py:689
  175.6 26.7 %mix_forward.1 = (f32[1024,2304]{1,0:T(8,128)}, f32[64,2048]{1,0:T(8,128)S(1)}, f32[64,1024]{1,0:T(8,128)S(1)}, f32[1024,128]{1,0:T(8,128)S(1)}, f32[64,128]{1,0...) custom-call(bf16[1024,1024]{1,0:T(8,128)(2,1)S(1)} %multiply_convert_fusion.4.normed_ref, ...), custom_call_target="tpu_custom_call" | custom-call | flops 9663676416 | bytes 16777216 | tf_op jit(solution)/shard_map/mix_forward/pallas_call | solution.py:217
  205.0 5.4 all-gather.26.cloned.1.call-done
  210.4 4.6 multiply_reduce_fusion.10
  216.1 30.2 %all-gather.28.cloned.1.call-done = bf16[2048,1024]{1,0:T(8,128)(2,1)} async-done(((bf16[512,1024]{1,0:T(8,128)(2,1)}), bf16[2048,1024]{1,0:T(8,128)(2,1)}) %all-gather.28.cloned.1.call-update) | async-done | bytes 4194320 | tf_op jit(solution)/shard_map/all_gather | solution.py:691
  246.3 3.3 multiply_reduce_fusion.15
  251.3 19.0 %all-gather.30.cloned.1.call-done = bf16[1024,1024]{1,0:T(8,128)(2,1)} async-done(((bf16[256,1024]{1,0:T(8,128)(2,1)}), bf16[1024,1024]{1,0:T(8,128)(2,1)}) %all-gather.30.cloned.1.call-update) | async-done | bytes 2097168 | tf_op jit(solution)/shard_map/all_gather | solution.py:692
  272.5 7.2 all_gather.102
  279.6 17.5 %fusion.71 = (f32[256]{0:T(256)S(1)}, f32[256,12672]{1,0:T(8,128)}) fusion(bf16[256,1024]{1,0:T(8,128)(2,1)S(1)} %all_gather.102, bf16[12672,1024]{1,0:T(8,128)(2,1)} %table_ref.1), kind=kOutput, calls=%fused_computation.217 | convolution fusion | flops 6647021568 | bytes 39453696 | tf_op jit(solution)/shard_map/dot_general | solution.py:60
  297.1 7.2 select_reduce_fusion
  304.3 5.1 all-gather.15
  309.9 5.1 all-gather.16
  315.5 5.1 all-gather.14
  321.2 7.5 all_gather.94
  328.6 17.5 %fusion.70 = (f32[256]{0:T(256)S(1)}, f32[256,12672]{1,0:T(8,128)}) fusion(bf16[256,1024]{1,0:T(8,128)(2,1)S(1)} %all_gather.94, bf16[12672,1024]{1,0:T(8,128)(2,1)} %table_ref.1), kind=kOutput, calls=%fused_computation.216 | convolution fusion | flops 6647021568 | bytes 39453696 | tf_op jit(solution)/shard_map/dot_general | solution.py:60
  346.2 7.1 select_reduce_fusion.1
  353.3 5.1 all-gather.12
  359.0 5.1 all-gather.13
  364.6 5.1 all-gather.11
  373.8 21.6 %while.20 = (s32[]{:T(128)}, f32[256]{0:T(256)}, f32[256]{0:T(256)}, f32[256]{0:T(256)}, f32[256]{0:T(256)}, /*index=5*/f32[256]{0:T(256)}, f32[256]{0:T(256)}, ...) while((s32[]{:T(128)}, f32[256]{0:T(256)}, ...), condition=%wide.region_14.15_spmd, body=%wide.region_13.14_spmd.sunk | while | flops 3586 | bytes 30865 | solution.py:43
  397.2 19.8 %fusion.2 = f32[256,1024]{1,0:T(8,128)} fusion(bf16[12672,1024]{1,0:T(8,128)(2,1)} %table_ref.1, f32[256,12672]{1,0:T(8,128)} %get-tuple-element.352, f32[256]{0:T(256)S(1)} %get-tuple-element.303, s32[256]{0:T(256)} %sub.148), kind=kOutput, calls=%fused_computation.25 | convolution fusion | flops 6663241728 | bytes 39979008 | tf_op jit(solution)/shard_map/dot_general | solution.py:60
  419.3 20.3 %fusion.1 = f32[256,1024]{1,0:T(8,128)} fusion(bf16[12672,1024]{1,0:T(8,128)(2,1)} %table_ref.1, f32[256,12672]{1,0:T(8,128)} %get-tuple-element.350, f32[256]{0:T(256)S(1)} %get-tuple-element.305, s32[256]{0:T(256)} %sub.144), kind=kOutput, calls=%fused_computation.24 | convolution fusion | flops 6663241728 | bytes 39979008 | tf_op jit(solution)/shard_map/dot_general | solution.py:60
  445.1 24.8 %reduce-scatter.14.cloned.1.call-done = f32[64,1024]{1,0:T(8,128)} async-done(((f32[256,1024]{1,0:T(8,128)}), f32[64,1024]{1,0:T(8,128)}) %reduce-scatter.14.cloned.1.call-update) | async-done | bytes 262160 | tf_op jit(solution)/shard_map/reduce_scatter | solution.py:743
  475.3 4.1 convolution_convert_fusion.1
  479.6 4.8 multiply_reduce_fusion.8
  487.2 3.3 convolution_convert_fusion.2
  492.7 45.3 %mix_backward.1 = (bf16[1024,2304]{1,0:T(8,128)(2,1)}, f32[5,2304]{1,0:T(8,128)S(1)}, f32[32,1024]{1,0:T(8,128)S(1)}, f32[32,128]{1,0:T(8,128)S(1)}) custom-call(f32[1024,2304]{1,0:T(8,128)} %get-tuple-element.105.input_ref, f32[5,2304]{1,0:T(8,128)S(1)} %bitcast.155, f32[64,2048]{1,0:T(8,128)S(1)} %get-tuple-element.318.grad_ref, f32[64,1024]{1,0:T(8,128)S(1)} %copy-done.4, ...), custom_call_target="tpu_custom_call" | custom-call | flops 3221225472 | bytes 20971520 | tf_op jit(solution)/shard_map/mix_backward/pallas_call | solution.py:414
  538.0 9.1 convolution_convert_fusion
  550.4 67.7 %all-gather = s32[32768]{0:T(1024)S(1)} all-gather(s32[1024]{0:T(1024)S(1)} %copy-done.9), channel_id=2, replica_groups=mesh['dp'=8,'fsdp'=4] {'fsdp','dp'}, dimensions={0}, use_global_device_ids=true | all-gather | bytes 135168 | tf_op jit(solution)/shard_map/all_gather | solution.py:670
  619.5 9.1 fusion.72
  628.7 3.5 multiply_reduce_fusion.2
  633.8 3.2 multiply_reduce_fusion.12
  637.1 11.9 %reduce-scatter.20.cloned.1.call-done = bf16[256,2304]{1,0:T(8,128)(2,1)} async-done(((bf16[1024,2304]{1,0:T(8,128)(2,1)}), bf16[256,2304]{1,0:T(8,128)(2,1)}) %reduce-scatter.20.cloned.1.call-update) | async-done | bytes 1179664 | tf_op jit(solution)/shard_map/reduce_scatter | solution.py:784
  649.3 5.9 fusion.11
  655.3 4.0 copy.137
  659.2 4.0 copy.138
  663.3 105.5 %all_to_all.15 = bf16[1,1024,8,128]{3,1,0,2:T(8,128)(2,1)} all-to-all(bf16[1,1024,8,128]{3,1,0,2:T(8,128)(2,1)} %copy.138), channel_id=1, replica_groups=mesh['dp'=8,'fsdp'=4] {'dp'}, dimensions={2} | all-to-all | bytes 4194304 | tf_op jit(solution)/shard_map/all_to_all | solution.py:832
  769.1 13.2 %all_gather.111 = f32[2,2048]{1,0:T(2,128)S(1)} all-gather(f32[2,512]{1,0:T(2,128)S(1)} %pad_maximum_fusion.5), channel_id=1, replica_groups={{0,8,16,24},{4,12,20,28},{1,9,17,25},{5,13,21,29},{2,10,18,26},{6,14,22..., dimensions={1}, use_global_device_ids=true | all-gather | bytes 20480 | tf_op jit(solution)/shard_map/all_gather | solution.py:799
  785.4 102.5 %table_grads.1 = (f32[12672,128]{1,0:T(8,128)}, bf16[12672,128]{1,0:T(8,128)(2,1)}) custom-call(s32[1]{0:T(128)} %bitcast.35.first_id_ref, bf16[12672,1024]{1,0:T(8,128)(2,1)} %table_ref.1, bf16[2048,1024]{1,0:T(8,128)(2,1)} %all-gather.32.cloned.1.call-done.rows_ref, bf16[2048,256]{1,0:T(8,128)(2,1)} %pad_maximum_fusion.2.columns_ref, ...), custom_call_target="tpu_custom_call" | custom-call | flops 66437775360 | bytes 35684352 | tf_op jit(solution)/shard_map/table_grads/pallas_call | solution.py:509
  896.7 3.7 fusion
  908.6 11.3 all-reduce.4
  924.4 40.3 %all-reduce.9.cloned.1.call-done = (bf16[256,2304]{1,0:T(8,128)(2,1)}, bf16[256,2048]{1,0:T(8,128)(2,1)}, bf16[512,1024]{1,0:T(8,128)(2,1)}, bf16[256,1024]{1,0:T(8,128)(2,1)}) async-done(((bf16[256,2304]{1,0:T(8,128)(2,1)}, bf16[256,2048]{1,0:T(8,128)(2,1)}, bf16[512,1024]{1,0:T(8,128)(2,1)}, bf16[256,1024]{1,0:T(8,128)(2,1)}), (bf16[256,2304]{1,0:T(8,128)(2,1)}, bf16[256,2048]{1,0:T(8,128)(2,1)}, ...) | async-done | bytes 3801104 | tf_op jit(solution)/shard_map/psum | solution.py:842
  972.6 4.8 collective-permute-done.other_ref
  977.4 45.6 %all-gather.34.cloned.1.call-done = bf16[32,1,1024,1,128]{4,2,3,1,0:T(8,128)(2,1)} async-done(((bf16[8,1,1024,1,128]{4,2,3,1,0:T(8,128)(2,1)}), bf16[32,1,1024,1,128]{4,2,3,1,0:T(8,128)(2,1)}) %all-gather.34.cloned.1.call-update) | async-done | bytes 8388624 | tf_op jit(solution)/shard_map/all_gather | solution.py:838
  1023.0 35.6 %token_grads.1 = f32[12672,128]{1,0:T(8,128)} custom-call(s32[32]{0:T(128)} %get-tuple-element.320.counts_ref, s32[32,1,1024]{2,1,0:T(1,128)} %broadcast_in_dim.34.listing_ref, bf16[32,1024,128]{2,1,0:T(8,128)(2,1)} %bitcast.158, f32[12672,128]{1,0:T(8,128)} %get-tuple-element.118.own_ref, bf16[12672,128]{1,0:T(8,128)(2,1)} %collective-permute-done.other_ref), custom_call_target="tpu_custom_call" | custom-call | flops 4194304 | bytes 67108864 | tf_op jit(solution)/shard_map/token_grads/pallas_call | solution.py:583
  1058.6 5.3 multiply_reduce_fusion
  1063.9 40.4 %all-reduce.10 = (f32[12672]{0:T(1024)S(1)}, f32[256,32]{1,0:T(8,128)S(1)}, f32[5,576]{1,0:T(8,128)}, f32[3,8]{0,1:T(8,128)}, f32[1024]{0:T(1024)S(1)}, /*index=5*/f32[1]{0:T(128)}, f32[]{:T(128)}) all-reduce(f32[12672]{0:T(1024)} %get-tuple-element.229, ...), channel_id=1, replica_groups=mesh['dp'=8,'fsdp'=4] {'dp'}, use_global_device_ids=true, to_apply=%region_22.23 | all-reduce | flops 24794 | bytes 198352 | tf_op jit(solution)/shard_map/psum | solution.py:871
  1108.1 3.5 multiply_reduce_fusion.6
  1111.6 12.2 %stack.84 = f32[18]{0:T(128)} concatenate(f32[1]{0:T(128)} %bitcast.37, f32[1]{0:T(128)} %bitcast.38, f32[1]{0:T(128)} %bitcast.39, f32[1]{0:T(128)} %bitcast.40, f32[1]{0:T(128)} %bitcast.41, f32[1]{0:T(128)} %bitcast.43, f32[1]{0:T(128)} %bitcast.44, f32[1]{0:T(128)} %get-tuple-element.281, f32[1]{0:T(128)} %bitcast.46, f32[1]{0:T(128)} %bitcast.47, f32[1]{0:T(128)} %bitcast.48, ...), dimensions={0} | concatenate | bytes 144 | tf_op jit(solution)/shard_map/stack | solution.py:875
  1123.8 15.8 %all-reduce.3 = (f32[18]{0:T(128)S(1)}, f32[128]{0:T(128)}, f32[4384]{0:T(1024)}, f32[1024]{0:T(1024)}, f32[1024]{0:T(1024)}) all-reduce(f32[18]{0:T(128)} %stack.84, f32[128]{0:T(128)} %get-tuple-element.228, f32[4384]{0:T(1024)} %get-tuple-element.233, f32[1024]{0:T(1024)} %get-tuple-element.236, ...), channel_id=1, replica_groups=mesh['dp'=8,'fsdp'=4] {'fsdp'}, use_global_device_ids=true, to_apply=%region_62.63 | all-reduce | flops 6578 | bytes 52624 | tf_op jit(solution)/shard_map/psum | solution.py:882
  1155.9 4.4 convert_subtract_fusion.1
  1160.4 6.0 copy.144
  1173.1 9.2 convert_subtract_fusion
  (378 shorter events, 131.8 us)
Async XLA Ops:
  8.0 125.6 %reduce-scatter.12.cloned.1.call-start = ((), (), s32[]{:S(2)}) async-start(), calls=%async_computation.10 | async-start | bytes 10485760 | tf_op jit(solution)/shard_map/reduce_scatter | solution.py:684
  60.2 113.0 %all-gather.24.cloned.1.call-start = ((), (), s32[]{:S(2)}) async-start(), calls=%async_computation.11 | async-start | bytes 5898240 | tf_op jit(solution)/shard_map/all_gather | solution.py:689
  64.5 12.2 %slice-start = ((bf16[256,4384]{0,1:T(8,128)(2,1)}), bf16[256,32]{0,1:T(8,128)(2,1)S(1)}, s32[]{:S(2)}) async-start(bf16[256,4384]{0,1:T(8,128)(2,1)} %param.27), calls=%async_computation.28 | async-start | bytes 32768 | tf_op jit(solution)/shard_map/slice | solution.py:690
  64.5 17.4 %copy-start.72 = (bf16[3,8]{1,0:T(4,128)(2,1)S(1)}, bf16[3,8]{1,0:T(4,128)(2,1)}, u32[]{:S(2)}) copy-start(bf16[3,8]{1,0:T(4,128)(2,1)} %param.31) | copy-start | bytes 148
  64.5 22.7 %copy-start.37 = (bf16[5,576]{1,0:T(8,128)(2,1)S(1)}, bf16[5,576]{1,0:T(8,128)(2,1)}, u32[]{:S(2)}) copy-start(bf16[5,576]{1,0:T(8,128)(2,1)} %param.30) | copy-start | bytes 17284
  66.9 143.5 %all-gather.26.cloned.1.call-start = ((), (), s32[]{:S(2)}) async-start(), calls=%async_computation.12 | async-start | bytes 5242880 | tf_op jit(solution)/shard_map/all_gather | solution.py:688
  69.4 176.9 %all-gather.28.cloned.1.call-start = ((), (), s32[]{:S(2)}) async-start(), calls=%async_computation.13 | async-start | bytes 5242880 | tf_op jit(solution)/shard_map/all_gather | solution.py:691
  70.0 200.3 %all-gather.30.cloned.1.call-start = ((), (), s32[]{:S(2)}) async-start(), calls=%async_computation.14 | async-start | bytes 2621440 | tf_op jit(solution)/shard_map/all_gather | solution.py:692
  70.6 371.4 %reduce-scatter.16.cloned.1.call-start = ((), (), s32[]{:S(2)}) async-start(), calls=%async_computation.16 | async-start | bytes 1310720 | tf_op jit(solution)/shard_map/reduce_scatter | solution.py:744
  81.9 65.1 %copy-start.32 = (bf16[1024,32]{0,1:T(8,128)(2,1)}, bf16[1024,32]{0,1:T(8,128)(2,1)S(1)}, u32[]{:S(2)}) copy-start(bf16[1024,32]{0,1:T(8,128)(2,1)S(1)} %all_gather.90) | copy-start | bytes 196612
  143.8 29.5 %copy-start.83 = (f32[64]{0:T(128)}, f32[64]{0:T(128)S(1)}, u32[]{:S(2)}) copy-start(f32[64]{0:T(128)S(1)} %multiply_reduce_fusion.16) | copy-start | bytes 772
  215.0 264.5 %copy-start.13 = (f32[64,2048]{1,0:T(8,128)}, f32[64,2048]{1,0:T(8,128)S(1)}, u32[]{:S(2)}) copy-start(f32[64,2048]{1,0:T(8,128)S(1)} %get-tuple-element.307) | copy-start | bytes 1572868
  279.6 17.5 %copy-start.27 = (bf16[256,1024]{1,0:T(8,128)(2,1)}, bf16[256,1024]{1,0:T(8,128)(2,1)S(1)}, u32[]{:S(2)}) copy-start(bf16[256,1024]{1,0:T(8,128)(2,1)S(1)} %all_gather.102) | copy-start | bytes 1572868
  279.6 17.5 %copy-start.64 = (s32[256]{0:T(256)S(1)}, s32[256]{0:T(256)}, u32[]{:S(2)}) copy-start(s32[256]{0:T(256)} %sub.148) | copy-start | bytes 3076
  297.1 24.1 %copy-start.26 = (bf16[64,1024]{1,0:T(8,128)(2,1)S(1)}, bf16[64,1024]{1,0:T(8,128)(2,1)}, u32[]{:S(2)}) copy-start(bf16[64,1024]{1,0:T(8,128)(2,1)} %multiply_convert_fusion.6) | copy-start | bytes 393220
  309.3 36.8 %copy-start.51 = (f32[4,1,256]{2,1,0:T(1,128)}, f32[4,1,256]{2,1,0:T(1,128)S(1)}, u32[]{:S(2)}) copy-start(f32[4,1,256]{2,1,0:T(1,128)S(1)} %all-gather.15) | copy-start | bytes 12292
  315.0 31.2 %copy-start.52 = (f32[4,1,256]{2,1,0:T(1,128)}, f32[4,1,256]{2,1,0:T(1,128)S(1)}, u32[]{:S(2)}) copy-start(f32[4,1,256]{2,1,0:T(1,128)S(1)} %all-gather.16) | copy-start | bytes 12292
  320.6 25.5 %copy-start.53 = (f32[4,1,256]{2,1,0:T(1,128)}, f32[4,1,256]{2,1,0:T(1,128)S(1)}, u32[]{:S(2)}) copy-start(f32[4,1,256]{2,1,0:T(1,128)S(1)} %all-gather.14) | copy-start | bytes 12292
  328.6 17.5 %copy-start.29 = (bf16[256,1024]{1,0:T(8,128)(2,1)}, bf16[256,1024]{1,0:T(8,128)(2,1)S(1)}, u32[]{:S(2)}) copy-start(bf16[256,1024]{1,0:T(8,128)(2,1)S(1)} %all_gather.94) | copy-start | bytes 1572868
  328.6 17.5 %copy-start.63 = (s32[256]{0:T(256)S(1)}, s32[256]{0:T(256)}, u32[]{:S(2)}) copy-start(s32[256]{0:T(256)} %sub.144) | copy-start | bytes 3076
  346.2 24.0 %slice-start.2 = ((f32[4,1,256]{2,1,0:T(1,128)}), f32[3,1,256]{2,1,0:T(1,128)S(1)}, s32[]{:S(2)}) async-start(f32[4,1,256]{2,1,0:T(1,128)} %copy-done.52), calls=%async_computation.30 | async-start | bytes 6144 | tf_op jit(solution)/shard_map/slice | solution.py:42
  346.2 24.6 %slice-start.1 = ((f32[4,1,256]{2,1,0:T(1,128)}), f32[3,1,256]{2,1,0:T(1,128)S(1)}, s32[]{:S(2)}) async-start(f32[4,1,256]{2,1,0:T(1,128)} %copy-done.51), calls=%async_computation.29 | async-start | bytes 6144 | tf_op jit(solution)/shard_map/slice | solution.py:42
  346.2 25.2 %slice-start.3 = ((f32[4,1,256]{2,1,0:T(1,128)}), f32[3,1,256]{2,1,0:T(1,128)S(1)}, s32[]{:S(2)}) async-start(f32[4,1,256]{2,1,0:T(1,128)} %copy-done.53), calls=%async_computation.31 | async-start | bytes 6144 | tf_op jit(solution)/shard_map/slice | solution.py:42
  417.0 52.9 %reduce-scatter.14.cloned.1.call-start = ((), (), s32[]{:S(2)}) async-start(), calls=%async_computation.15 | async-start | bytes 1310720 | tf_op jit(solution)/shard_map/reduce_scatter | solution.py:743
  439.6 197.4 %reduce-scatter.26.cloned.1.call-start = ((), (), s32[]{:S(2)}) async-start(), calls=%async_computation.22 | async-start | bytes 2621440 | tf_op jit(solution)/shard_map/reduce_scatter | solution.py:784
  445.0 192.0 %reduce-scatter.24.cloned.1.call-start = ((), (), s32[]{:S(2)}) async-start(), calls=%async_computation.21 | async-start | bytes 5242880 | tf_op jit(solution)/shard_map/reduce_scatter | solution.py:784
  479.5 157.6 %reduce-scatter.18.cloned.1.call-start = ((), (), s32[]{:S(2)}) async-start(), calls=%async_computation.18 | async-start | bytes 5242880 | tf_op jit(solution)/shard_map/reduce_scatter | solution.py:784
  490.5 158.5 %reduce-scatter.20.cloned.1.call-start = ((), (), s32[]{:S(2)}) async-start(), calls=%async_computation.19 | async-start | bytes 5898240 | tf_op jit(solution)/shard_map/reduce_scatter | solution.py:784
  547.1 235.8 %all-gather.32.cloned.1.call-start = ((), (), s32[]{:S(2)}) async-start(), calls=%async_computation.17 | async-start | bytes 5242880 | tf_op jit(solution)/shard_map/all_gather | solution.py:796
  550.3 355.3 %sort.9.cloned.1.call-start = ((), (), s32[]{:S(2)}) async-start(), calls=%async_computation.26 | async-start | bytes 393248 | tf_op jit(solution)/shard_map/sort | solution.py:674
  619.5 303.2 %reduce-scatter.28.cloned.1.call-start = ((), (), s32[]{:S(2)}) async-start(), calls=%async_computation.24 | async-start | bytes 1474560
  633.7 15.7 %copy-start.23 = (f32[64,1024]{1,0:T(8,128)S(1)}, f32[64,1024]{1,0:T(8,128)}, u32[]{:S(2)}) copy-start(f32[64,1024]{1,0:T(8,128)} %copy-done.22) | copy-start | bytes 786436
  633.7 15.7 %copy-start.82 = (s32[64]{0:T(128)S(1)}, s32[64]{0:T(128)}, u32[]{:S(2)}) copy-start(s32[64]{0:T(128)} %get-tuple-element.344) | copy-start | bytes 772
  633.7 331.0 %all-reduce.9.cloned.1.call-start = ((), (), s32[]{:S(2)}) async-start(), calls=%async_computation.25 | async-start | bytes 7602176 | tf_op jit(solution)/shard_map/psum | solution.py:842
  649.1 374.0 %all-gather.34.cloned.1.call-start = ((), (), s32[]{:S(2)}) async-start(), calls=%async_computation.23 | async-start | bytes 10485760 | tf_op jit(solution)/shard_map/all_gather | solution.py:838
  659.2 109.6 %copy-start.57 = (s32[4,64]{1,0:T(4,128)S(1)}, s32[4,64]{1,0:T(4,128)}, u32[]{:S(2)}) copy-start(s32[4,64]{1,0:T(4,128)} %get-tuple-element.321) | copy-start | bytes 3076
  659.2 109.7 %copy-start.56 = (s32[4,64]{1,0:T(4,128)S(1)}, s32[4,64]{1,0:T(4,128)}, u32[]{:S(2)}) copy-start(s32[4,64]{1,0:T(4,128)} %get-tuple-element.324) | copy-start | bytes 3076
  659.2 109.8 %copy-start.77 = (f32[256]{0:T(256)S(1)}, f32[256]{0:T(256)}, u32[]{:S(2)}) copy-start(f32[256]{0:T(256)} %copy-done.76) | copy-start | bytes 3076
  659.2 109.8 %copy-start.79 = (f32[256]{0:T(256)S(1)}, f32[256]{0:T(256)}, u32[]{:S(2)}) copy-start(f32[256]{0:T(256)} %copy-done.78) | copy-start | bytes 3076
  768.8 295.1 %reduce-scatter.22.cloned.1.call-start = ((), (), s32[]{:S(2)}) async-start(), calls=%async_computation.20 | async-start | bytes 655360 | tf_op jit(solution)/shard_map/reduce_scatter | solution.py:788
  785.3 104.1 %copy-start.73 = (bf16[3,8]{1,0:T(4,128)(2,1)S(1)}, bf16[3,8]{1,0:T(4,128)(2,1)}, u32[]{:S(2)}) copy-start(bf16[3,8]{1,0:T(4,128)(2,1)} %param.31) | copy-start | bytes 148
  785.3 104.2 %copy-start.89 = (u32[32]{0:T(128)S(1)}, u32[32]{0:T(128)}, u32[]{:S(2)}) copy-start(u32[32]{0:T(128)} %constant.216) | copy-start | bytes 388
  785.3 106.0 %copy-start.35 = (f32[12672]{0:T(1024)S(1)}, f32[12672]{0:T(1024)}, u32[]{:S(2)}) copy-start(f32[12672]{0:T(1024)} %param.33) | copy-start | bytes 152068
  785.3 106.7 %copy-start.75 = (f32[256]{0:T(256)S(1)}, f32[256]{0:T(256)}, u32[]{:S(2)}) copy-start(f32[256]{0:T(256)} %param.35) | copy-start | bytes 3076
  785.3 107.4 %copy-start.58 = (f32[512]{0:T(512)S(1)}, f32[512]{0:T(512)}, u32[]{:S(2)}) copy-start(f32[512]{0:T(512)} %param.37) | copy-start | bytes 6148
  785.4 108.0 %copy-start.74 = (f32[256]{0:T(256)S(1)}, f32[256]{0:T(256)}, u32[]{:S(2)}) copy-start(f32[256]{0:T(256)} %param.39) | copy-start | bytes 3076
  785.4 108.7 %copy-start.81 = (f32[3,8]{1,0:T(4,128)S(1)}, f32[3,8]{1,0:T(4,128)}, u32[]{:S(2)}) copy-start(f32[3,8]{1,0:T(4,128)} %param.42) | copy-start | bytes 292
  785.4 109.4 %copy-start.46 = (bf16[1024]{0:T(1024)(128)(2,1)S(1)}, bf16[1024]{0:T(1024)(128)(2,1)}, u32[]{:S(2)}) copy-start(bf16[1024]{0:T(1024)(128)(2,1)} %param.32) | copy-start | bytes 6148
  785.4 110.6 %copy-start.38 = (bf16[5,576]{1,0:T(8,128)(2,1)S(1)}, bf16[5,576]{1,0:T(8,128)(2,1)}, u32[]{:S(2)}) copy-start(bf16[5,576]{1,0:T(8,128)(2,1)} %param.30) | copy-start | bytes 17284
  785.4 115.0 %copy-start.18 = (bf16[256,1024]{1,0:T(8,128)(2,1)S(1)}, bf16[256,1024]{1,0:T(8,128)(2,1)}, u32[]{:S(2)}) copy-start(bf16[256,1024]{1,0:T(8,128)(2,1)} %param.29) | copy-start | bytes 1572868
  888.0 20.6 %copy-start.43 = (f32[2048]{0:T(1024)S(1)}, f32[2048]{0:T(1024)}, u32[]{:S(2)}) copy-start(f32[2048]{0:T(1024)} %get-tuple-element.238) | copy-start | bytes 24580
  888.0 20.6 %copy-start.48 = (f32[1024]{0:T(1024)S(1)}, f32[1024]{0:T(1024)}, u32[]{:S(2)}) copy-start(f32[1024]{0:T(1024)} %get-tuple-element.245) | copy-start | bytes 12292
  888.0 89.5 %collective-permute-start = (bf16[12672,128]{1,0:T(8,128)(2,1)}, bf16[12672,128]{1,0:T(8,128)(2,1)}, u32[]{:S(2)}, u32[]{:S(2)}) collective-permute-start(bf16[12672,128]{1,0:T(8,128)(2,1)} %get-tuple-element.119), channel_id=1, source_target_pairs={{0,4},{4,0},{8,12},{12,8},{16,20},{20,16},{24,28},{28,24},{1,5},{5... | collective-permute-start | bytes 9732104 | tf_op jit(solution)/shard_map/ppermute | solution.py:829
  1058.6 97.4 %copy-start.12 = (bf16[256,4384]{1,0:T(8,128)(2,1)S(1)}, bf16[256,4384]{1,0:T(8,128)(2,1)}, u32[]{:S(2)}) copy-start(bf16[256,4384]{1,0:T(8,128)(2,1)} %copy.129) | copy-start | bytes 6733828
  1104.2 19.6 %copy-start.49 = (f32[1024]{0:T(1024)}, f32[1024]{0:T(1024)S(1)}, u32[]{:S(2)}) copy-start(f32[1024]{0:T(1024)S(1)} %get-tuple-element.280) | copy-start | bytes 12292
  1104.2 41.5 %copy-start.36 = (f32[12672]{0:T(1024)}, f32[12672]{0:T(1024)S(1)}, u32[]{:S(2)}) copy-start(f32[12672]{0:T(1024)S(1)} %get-tuple-element.276) | copy-start | bytes 152068
  1146.7 26.4 %copy-start.34 = (f32[12672]{0:T(1024)}, f32[12672]{0:T(1024)S(1)}, u32[]{:S(2)}) copy-start(f32[12672]{0:T(1024)S(1)} %multiply_add_fusion.2) | copy-start | bytes 152068
  1147.4 22.4 %copy-start.65 = (f32[256]{0:T(256)}, f32[256]{0:T(256)S(1)}, u32[]{:S(2)}) copy-start(f32[256]{0:T(256)S(1)} %multiply_add_fusion.8) | copy-start | bytes 3076
  1150.1 21.0 %copy-start.55 = (f32[512]{0:T(512)}, f32[512]{0:T(512)S(1)}, u32[]{:S(2)}) copy-start(f32[512]{0:T(512)S(1)} %multiply_add_fusion.7) | copy-start | bytes 6148
  1160.4 10.7 copy-start.17
  1160.4 10.7 copy-start.21
  1169.6 12.6 %copy-start.47 = (f32[1024]{0:T(1024)}, f32[1024]{0:T(1024)S(1)}, u32[]{:S(2)}) copy-start(f32[1024]{0:T(1024)S(1)} %multiply_add_fusion.4) | copy-start | bytes 12292
  1169.7 12.5 %copy-start.54 = (f32[1024]{0:T(1024)}, f32[1024]{0:T(1024)S(1)}, u32[]{:S(2)}) copy-start(f32[1024]{0:T(1024)S(1)} %multiply_add_fusion.5) | copy-start | bytes 12292
  1169.7 12.5 %copy-start.80 = (f32[128]{0:T(128)}, f32[128]{0:T(128)S(1)}, u32[]{:S(2)}) copy-start(f32[128]{0:T(128)S(1)} %multiply_add_fusion.10) | copy-start | bytes 1540
  (48 other events, 213.0 us)
Sparse Core Ops, SparseCore 0:
  60.3 73.2 reduce-scatter.11
  135.8 37.4 all-gather.23
  175.4 34.9 all-gather.25
  211.8 34.4 all-gather.27
  247.7 22.5 all-gather.29
  417.1 24.7 reduce-scatter.15
  445.0 24.7 reduce-scatter.13
  472.9 31.1 reduce-scatter.25
  506.7 44.5 reduce-scatter.23
  553.7 44.7 reduce-scatter.17
  601.0 47.9 reduce-scatter.19
  651.0 125.3 all-gather.31
  779.0 23.9 reduce-scatter.27
  806.9 157.7 all-reduce.8
  966.1 56.8 all-gather.33
  1025.9 21.6 reduce-scatter.21
Sparse Core Ops, SparseCore 1:
  619.6 6.8 sort.11.cloned.1.call-done
  (1 shorter events, 0.0 us)
